TPU v7x, 128 devices: a whole 4x4x4 slice. The times are simulated.
128 devices in a mesh: data: 1, chip: 16 (over z, y), dap: 8 (over x, core).
Axes of the slice: x: 4, y: 4, z: 4, core: 2. Of those that a mesh axis runs over, the one named last changes fastest.
Arguments:
- m: bfloat16 [256, 512, 256], P(('data', 'chip', 'dap'))
- z: bfloat16 [512, 512, 128], P(('data', 'chip', 'dap'))
- msa_mask: int32 [256, 512], P('data')
- res_mask: int32 [512], P('data')
- w_row_in: bfloat16 [256, 1024], replicated
- w_row_bias: bfloat16 [128, 8], replicated
- w_row_out: bfloat16 [256, 256], replicated
- w_col_in: bfloat16 [256, 1024], replicated
- w_col_out: bfloat16 [256, 256], replicated
- w_opm_in: bfloat16 [256, 64], replicated
- w_opm_out: bfloat16 [1024, 128], replicated
- w_start_in: bfloat16 [128, 512], replicated
- w_start_bias: bfloat16 [128, 4], replicated
- w_start_out: bfloat16 [128, 128], replicated
- w_end_in: bfloat16 [128, 512], replicated
- w_end_bias: bfloat16 [128, 4], replicated
- w_end_out: bfloat16 [128, 128], replicated
Outputs:
- output 1: bfloat16 [256, 512, 256], P(('data', 'chip', 'dap'))
- output 2: bfloat16 [512, 512, 128], P(('data', 'chip', 'dap'))
All inputs are finite; a program needn't handle non-finite values.
Results may differ from a plain program's by a relative error of at most 0.0123337.
Values are sent between devices in bfloat16 or wider.
A program may use at most 1 GiB of HBM per device.

v0:
```python
import jax
import jax.numpy as jnp
from jax import lax
from jax.sharding import PartitionSpec as P


def layer_norm(x):
    values = x.astype(jnp.float32)
    centred = values - jnp.mean(values, axis=-1, keepdims=True)
    variance = jnp.mean(centred * centred, axis=-1, keepdims=True)
    return (centred * lax.rsqrt(variance + 1e-5)).astype(jnp.bfloat16)


def add_residual(state, update):
    return (state.astype(jnp.float32) + update).astype(jnp.bfloat16)


def gated_attention(x_norm, w_in, w_out, heads, head_bias, key_ok, along_first):
    width = x_norm.shape[-1]
    head_dim = w_out.shape[0] // heads
    w_heads = jnp.transpose(w_in.reshape(width, 4, heads, head_dim), (2, 0, 1, 3))
    w_back = w_out.reshape(heads, head_dim, w_out.shape[1])
    if along_first:
        forms = ('nbc,cfd->nbfd', 'ibd,jbd->bij', 'bij,jbd->ibd', 'hibd,hdc->ibc')
    else:
        forms = ('bnc,cfd->bnfd', 'bid,bjd->bij', 'bij,bjd->bid', 'hbid,hdc->bic')
    key_keep = key_ok[:, None, :]
    scale = head_dim ** -0.5

    def one_head(head_in):
        projected = jnp.einsum(forms[0], x_norm, head_in[0], preferred_element_type=jnp.float32).astype(jnp.bfloat16)
        scores = jnp.einsum(forms[1], projected[:, :, 0], projected[:, :, 1], preferred_element_type=jnp.float32) * scale
        if len(head_in) > 1:
            scores = scores + head_in[1].astype(jnp.float32)[None]
        scores = jnp.where(key_keep, scores, -1e9)
        attn_prob = jax.nn.softmax(scores, axis=-1).astype(jnp.bfloat16)
        mixed = jnp.einsum(forms[2], attn_prob, projected[:, :, 2], preferred_element_type=jnp.float32)
        return (mixed * jax.nn.sigmoid(projected[:, :, 3].astype(jnp.float32))).astype(jnp.bfloat16)

    head_in = (w_heads,) if head_bias is None else (w_heads, head_bias)
    gated = lax.map(one_head, head_in)
    return jnp.einsum(forms[3], gated, w_back, preferred_element_type=jnp.float32)


def solution(mesh):
    dap_size = mesh.shape['dap']
    group = ('chip', 'dap')
    rows = P(('data', 'chip', 'dap'))
    in_specs = (rows, rows, P('data'), P('data')) + (P(),) * 13

    def per_device(m_blk, z_blk, value_a8, res_mask, w_row_in, w_row_bias, w_row_out, w_col_in, w_col_out,
                   w_opm_in, w_opm_out, w_start_in, w_start_bias, w_start_out, w_end_in, w_end_bias, w_end_out):
        group_idx = lax.axis_index('chip') * dap_size + lax.axis_index('dap')
        seq_loc = m_blk.shape[0]
        res_loc = z_blk.shape[0]
        heads_m = w_row_bias.shape[1]
        heads_t = w_start_bias.shape[1]
        opm = w_opm_in.shape[1] // 2
        value_a6 = value_a8 != 0
        res_ok = (res_mask != 0)[None, :]

        row_bias = jnp.einsum('ijc,ch->hij', layer_norm(z_blk), w_row_bias, preferred_element_type=jnp.float32).astype(jnp.bfloat16)
        row_bias = lax.all_gather(row_bias, group, axis=1, tiled=True)
        seq_ok = lax.dynamic_slice_in_dim(value_a6, group_idx * seq_loc, seq_loc, axis=0)
        m_blk = add_residual(m_blk, gated_attention(layer_norm(m_blk), w_row_in, w_row_out, heads_m, row_bias, seq_ok, False))

        m_cols = lax.all_to_all(m_blk, group, 1, 0, tiled=True)
        col_mask = lax.dynamic_slice_in_dim(value_a8, group_idx * res_loc, res_loc, axis=1)
        m_cols = add_residual(m_cols, gated_attention(layer_norm(m_cols), w_col_in, w_col_out, heads_m, None, (col_mask != 0).T, True))

        outer_proj = jnp.dot(layer_norm(m_cols), w_opm_in, preferred_element_type=jnp.float32).astype(jnp.bfloat16)
        col_w = col_mask.astype(jnp.bfloat16)
        left = outer_proj[:, :, :opm] * col_w[:, :, None]
        right = lax.all_gather(outer_proj[:, :, opm:] * col_w[:, :, None], group, axis=1, tiled=True)
        pair_norm = jnp.einsum('si,sj->ij', col_w, value_a8.astype(jnp.bfloat16), preferred_element_type=jnp.float32)
        outer = jnp.einsum('sia,sjc->ijac', left, right, preferred_element_type=jnp.float32).astype(jnp.bfloat16)
        outer = outer.reshape(res_loc, outer.shape[1], opm * opm)
        z_blk = add_residual(z_blk, jnp.dot(outer, w_opm_out, preferred_element_type=jnp.float32) / (1e-3 + pair_norm[:, :, None]))

        start_norm = layer_norm(z_blk)
        start_bias = jnp.einsum('jkc,ch->hjk', start_norm, w_start_bias, preferred_element_type=jnp.float32).astype(jnp.bfloat16)
        start_bias = lax.all_gather(start_bias, group, axis=1, tiled=True)
        z_blk = add_residual(z_blk, gated_attention(start_norm, w_start_in, w_start_out, heads_t, start_bias, res_ok, False))

        z_cols = lax.all_to_all(z_blk, group, 1, 0, tiled=True)
        end_norm = layer_norm(z_cols)
        end_bias = jnp.einsum('kjc,ch->hjk', end_norm, w_end_bias, preferred_element_type=jnp.float32).astype(jnp.bfloat16)
        end_bias = lax.all_gather(end_bias, group, axis=1, tiled=True)
        z_cols = add_residual(z_cols, gated_attention(end_norm, w_end_in, w_end_out, heads_t, end_bias, res_ok, True))

        z_out = lax.all_to_all(z_cols, group, 0, 1, tiled=True)
        m_out = lax.all_to_all(m_cols, group, 0, 1, tiled=True)
        return m_out, z_out

    return jax.shard_map(per_device, mesh=mesh, in_specs=in_specs, out_specs=(rows, rows), check_vma=False)
```

profile of v0, /device:TPU:1, one launch (start us, length us, event | category | flops | bytes accessed | tf_op | source)
XLA Modules:
  0.0 515.8 jit_solution(13381572928077914906)
XLA Ops:
  14.2 67.3 %all-gather.5.cloned.1.call-done = bf16[8,512,512]{2,0,1:T(8,128)(2,1)} async-done(((bf16[8,4,512]{2,0,1:T(8,128)(2,1)}), bf16[8,512,512]{2,0,1:T(8,128)(2,1)}) %all-gather.5.cloned.1.call-update) | async-done | bytes 4194320 | tf_op jit(solution)/shard_map/all_gather | solution.py:63
  81.5 7.6 %copy.160 = bf16[8,512,512]{1,2,0:T(8,128)(2,1)} copy(bf16[8,512,512]{2,0,1:T(8,128)(2,1)} %all-gather.5.cloned.1.call-done) | data formatting | bytes 8388608 | tf_op jit(solution)/shard_map/while | solution.py:41
  89.1 40.6 %while.40 = (s32[]{:T(128)}, bf16[8,2,512,32]{2,3,1,0:T(8,128)(2,1)}, pred[2,1,512]{2,0,1:T(4,128)(4,1)S(1)}, bf16[8,256,4,32]{1,3,0,2:T(8,128)(2,1)}, bf16[2,51...) while((s32[]{:T(128)}, bf16[8,2,512,32]{2,3,1,0:T(8,128)(2,1)}, ...), condition=%wide.region_7.8_spmd, body=%wide.region_4.7_spmd.sunk | while | flops 174131200 | bytes 4993105 | solution.py:41
  132.4 5.3 %all-to-all-start = ((bf16[2,512,256]{2,0,1:T(2,128)(2,1)}), bf16[2,512,256]{2,0,1:T(2,128)(2,1)S(1)}, u32[]{:S(2)}, u32[]{:S(2)}) async-start(bf16[2,512,256]{2,0,1:T(2,128)(2,1)} %copy.161), calls=%async_computation | async-start | bytes 1048576 | tf_op jit(solution)/shard_map/all_to_all | solution.py:67
  139.1 12.0 %all-to-all-done = bf16[2,512,256]{2,0,1:T(2,128)(2,1)S(1)} async-done(((bf16[2,512,256]{2,0,1:T(2,128)(2,1)}), bf16[2,512,256]{2,0,1:T(2,128)(2,1)S(1)}, u32[]{:S(2)}, u32[]{:S(2)}) %all-to-all-start) | async-done | bytes 524320 | tf_op jit(solution)/shard_map/all_to_all | solution.py:67
  154.0 17.6 %while.41 = (s32[]{:T(128)}, bf16[8,256,4,32]{1,3,2,0:T(8,128)(2,1)}, bf16[8,256,4,32]{1,3,0,2:T(8,128)(2,1)S(1)}, bf16[256,4,256]{2,0,1:T(8,128)(2,1)S(1)}, pred[4,1,256]{2,0,1:T(4,128)(4,1)S(1)}, /*index=5*/s32[]{:T(128)}) while((s32[]{:T(128)}, bf16[8,256,4,32]{1,3,2,0:T(8,128)(2,1)}, bf16[8,256,4,32]{1,3,0,2:T(8,128)(2,1)S(1)}, ...), condition=%wide.region_13.14_spmd, body=%wide.region_10.13_spmd.sunk | while | flops 120129024 | bytes 1321545 | solution.py:41
  176.3 66.0 %all-gather.7.cloned.1.call-done = bf16[256,512,32]{0,2,1:T(8,128)(2,1)} async-done(((bf16[256,4,32]{0,2,1:T(8,128)(2,1)}), bf16[256,512,32]{0,2,1:T(8,128)(2,1)}) %all-gather.7.cloned.1.call-update) | async-done | bytes 8388624 | tf_op jit(solution)/shard_map/all_gather | solution.py:74
  242.3 13.3 %convert_bitcast_fusion = bf16[4,512,32,32]{1,2,0,3:T(8,128)(2,1)S(1)} fusion(bf16[256,512,32,1]{0,2,1,3:T(8,128)(2,1)} %bitcast.460, bf16[256,4,64]{0,2,1:T(8,128)(2,1)S(1)} %convolution_convert_fusion.4, bf16[256,4]{0,1:T(4,128)(2,1)S(1)} %convert_element_type.206), kind=kOutput, calls=%fused_computation.116 | convolution fusion | flops 1075970048 | bytes 12650496 | tf_op jit(solution)/shard_map/sia,sjc->ijac/dot_general | solution.py:76
  260.7 62.6 %all-gather.9.cloned.1.call-done = bf16[4,512,512]{2,0,1:T(4,128)(2,1)} async-done(((bf16[4,4,512]{2,0,1:T(4,128)(2,1)}), bf16[4,512,512]{2,0,1:T(4,128)(2,1)}) %all-gather.9.cloned.1.call-update) | async-done | bytes 2097168 | tf_op jit(solution)/shard_map/all_gather | solution.py:82
  323.4 4.3 copy.179
  327.7 31.5 %while.42 = (s32[]{:T(128)}, bf16[4,4,512,32]{2,3,1,0:T(8,128)(2,1)S(1)}, pred[1,1,512]{2,1,0:T(4,128)(4,1)S(1)}, bf16[4,128,4,32]{1,3,0,2:T(8,128)(2,1)S(1)}, b...) while((s32[]{:T(128)}, ...), condition=%wide.region_21.22_spmd, body=%wide.region_18.21_spmd.sunk | while | flops 209584640 | bytes 12764770 | solution.py:41
  329.2 3.7 fusion.186
  337.0 3.7 fusion.186
  340.7 2.7 fusion.187
  344.9 3.7 fusion.186
  352.8 3.7 fusion.186
  356.5 2.7 fusion.187
  359.9 18.7 %all_to_all.54 = bf16[4,512,128]{2,0,1:T(4,128)(2,1)S(1)} all-to-all(bf16[4,512,128]{2,0,1:T(4,128)(2,1)S(1)} %copy.181), channel_id=1, replica_groups=mesh['data'=1,'chip'=16,'dap'=8] {'chip','dap'}, dimensions={1} | all-to-all | bytes 1048576 | tf_op jit(solution)/shard_map/all_to_all | solution.py:85
  387.5 5.9 %all-to-all-start.1 = ((bf16[256,4,256]{2,1,0:T(4,128)(2,1)}), bf16[256,4,256]{2,1,0:T(4,128)(2,1)}, u32[]{:S(2)}, u32[]{:S(2)}) async-start(bf16[256,4,256]{2,1,0:T(4,128)(2,1)} %copy.168), calls=%async_computation.1 | async-start | bytes 1048576 | tf_op jit(solution)/shard_map/all_to_all | solution.py:92
  393.4 54.8 %all-gather.11.cloned.1.call-done = bf16[4,512,512]{2,0,1:T(4,128)(2,1)} async-done(((bf16[4,4,512]{2,0,1:T(4,128)(2,1)}), bf16[4,512,512]{2,0,1:T(4,128)(2,1)}) %all-gather.11.cloned.1.call-update) | async-done | bytes 2097168 | tf_op jit(solution)/shard_map/all_gather | solution.py:88
  448.2 4.3 copy.191
  452.4 34.1 %while.43 = (s32[]{:T(128)}, bf16[4,512,4,32]{1,3,2,0:T(8,128)(2,1)}, bf16[4,128,4,32]{1,3,0,2:T(8,128)(2,1)S(1)}, bf16[512,4,128]{2,0,1:T(8,128)(2,1)S(1)}, pre...) while((s32[]{:T(128)}, bf16[4,512,4,32]{1,3,2,0:T(8,128)(2,1)}, ...), condition=%wide.region_27.28_spmd, body=%wide.region_24.27_spmd.sunk | while | flops 209584640 | bytes 12765278 | solution.py:41
  453.9 3.7 fusion.191
  457.6 3.3 fusion.192
  462.5 3.7 fusion.191
  466.1 3.3 fusion.192
  471.0 3.7 fusion.191
  474.7 3.3 fusion.192
  479.5 3.7 fusion.191
  483.2 3.3 fusion.192
  489.1 5.3 %all-to-all-start.3 = ((bf16[512,4,128]{2,1,0:T(4,128)(2,1)}), bf16[512,4,128]{2,1,0:T(4,128)(2,1)S(1)}, u32[]{:S(2)}, u32[]{:S(2)}) async-start(bf16[512,4,128]{2,1,0:T(4,128)(2,1)} %copy.192), calls=%async_computation.3 | async-start | bytes 1048576 | tf_op jit(solution)/shard_map/all_to_all | solution.py:91
  496.8 11.1 %all-to-all-done.3 = bf16[512,4,128]{2,1,0:T(4,128)(2,1)S(1)} async-done(((bf16[512,4,128]{2,1,0:T(4,128)(2,1)}), bf16[512,4,128]{2,1,0:T(4,128)(2,1)S(1)}, u32[]{:S(2)}, u32[]{:S(2)}) %all-to-all-start.3) | async-done | bytes 524320 | tf_op jit(solution)/shard_map/all_to_all | solution.py:91
  (192 shorter events, 114.0 us)
Async XLA Ops:
  7.2 251.0 %copy-start = (bf16[1024,128]{1,0:T(8,128)(2,1)S(1)}, bf16[1024,128]{1,0:T(8,128)(2,1)}, u32[]{:S(2)}) copy-start(bf16[1024,128]{1,0:T(8,128)(2,1)} %param.35) | copy-start | bytes 786436
  7.2 6.0 %copy-start.4 = (bf16[2,512,256]{2,1,0:T(8,128)(2,1)S(1)}, bf16[2,512,256]{2,1,0:T(8,128)(2,1)}, u32[]{:S(2)}) copy-start(bf16[2,512,256]{2,1,0:T(8,128)(2,1)} %param.25) | copy-start | bytes 1572868
  7.2 74.3 %all-gather.5.cloned.1.call-start = ((), (), s32[]{:S(2)}) async-start(), calls=%async_computation.4 | async-start | bytes 4227072 | tf_op jit(solution)/shard_map/all_gather | solution.py:63
  89.1 40.6 %copy-start.13 = (bf16[256,256]{1,0:T(8,128)(2,1)S(1)}, bf16[256,256]{1,0:T(8,128)(2,1)}, u32[]{:S(2)}) copy-start(bf16[256,256]{1,0:T(8,128)(2,1)} %param.31) | copy-start | bytes 393220
  129.7 9.2 %copy-start.6 = (bf16[256,1024]{1,0:T(8,128)(2,1)S(1)}, bf16[256,1024]{1,0:T(8,128)(2,1)}, u32[]{:S(2)}) copy-start(bf16[256,1024]{1,0:T(8,128)(2,1)} %param.32) | copy-start | bytes 1572868
  132.4 18.7 %all-to-all-start = ((bf16[2,512,256]{2,0,1:T(2,128)(2,1)}), bf16[2,512,256]{2,0,1:T(2,128)(2,1)S(1)}, u32[]{:S(2)}, u32[]{:S(2)}) async-start(bf16[2,512,256]{2,0,1:T(2,128)(2,1)} %copy.161), calls=%async_computation | async-start | bytes 1048576 | tf_op jit(solution)/shard_map/all_to_all | solution.py:67
  137.7 104.6 %all-gather.7.cloned.1.call-start = ((), (), s32[]{:S(2)}) async-start(), calls=%async_computation.5 | async-start | bytes 8454144 | tf_op jit(solution)/shard_map/all_gather | solution.py:74
  154.0 18.0 %copy-start.7 = (bf16[256,256]{1,0:T(8,128)(2,1)S(1)}, bf16[256,256]{1,0:T(8,128)(2,1)}, u32[]{:S(2)}) copy-start(bf16[256,256]{1,0:T(8,128)(2,1)} %param.33) | copy-start | bytes 393220
  171.6 4.5 copy-start.5
  173.4 0.8 copy-start.2
  175.9 147.5 %all-gather.9.cloned.1.call-start = ((), (), s32[]{:S(2)}) async-start(), calls=%async_computation.6 | async-start | bytes 2113536 | tf_op jit(solution)/shard_map/all_gather | solution.py:82
  258.2 1.2 copy-start.11
  258.2 2.1 copy-start.10
  258.2 2.1 copy-start.8
  260.2 187.9 %all-gather.11.cloned.1.call-start = ((), (), s32[]{:S(2)}) async-start(), calls=%async_computation.7 | async-start | bytes 2113536 | tf_op jit(solution)/shard_map/all_gather | solution.py:88
  327.7 31.5 %copy-start.9 = (bf16[128,128]{1,0:T(8,128)(2,1)S(1)}, bf16[128,128]{1,0:T(8,128)(2,1)}, u32[]{:S(2)}) copy-start(bf16[128,128]{1,0:T(8,128)(2,1)} %param.38) | copy-start | bytes 98308
  379.3 5.2 %copy-start.12 = (bf16[128,4]{0,1:T(4,128)(2,1)S(1)}, bf16[128,4]{0,1:T(4,128)(2,1)}, u32[]{:S(2)}) copy-start(bf16[128,4]{0,1:T(4,128)(2,1)} %param.40) | copy-start | bytes 3076
  379.4 7.0 %copy-start.3 = (bf16[256,4,256]{0,2,1:T(8,128)(2,1)S(1)}, bf16[256,4,256]{0,2,1:T(8,128)(2,1)}, u32[]{:S(2)}) copy-start(bf16[256,4,256]{0,2,1:T(8,128)(2,1)} %copy-done.2) | copy-start | bytes 1572868
  387.5 101.6 %all-to-all-start.1 = ((bf16[256,4,256]{2,1,0:T(4,128)(2,1)}), bf16[256,4,256]{2,1,0:T(4,128)(2,1)}, u32[]{:S(2)}, u32[]{:S(2)}) async-start(bf16[256,4,256]{2,1,0:T(4,128)(2,1)} %copy.168), calls=%async_computation.1 | async-start | bytes 1048576 | tf_op jit(solution)/shard_map/all_to_all | solution.py:92
  486.5 22.3 %copy-start.1 = (bf16[1024,128]{1,0:T(8,128)(2,1)S(1)}, bf16[1024,128]{1,0:T(8,128)(2,1)}, u32[]{:S(2)}) copy-start(bf16[1024,128]{1,0:T(8,128)(2,1)} %param.35) | copy-start | bytes 786436
  489.1 18.7 %all-to-all-start.3 = ((bf16[512,4,128]{2,1,0:T(4,128)(2,1)}), bf16[512,4,128]{2,1,0:T(4,128)(2,1)S(1)}, u32[]{:S(2)}, u32[]{:S(2)}) async-start(bf16[512,4,128]{2,1,0:T(4,128)(2,1)} %copy.192), calls=%async_computation.3 | async-start | bytes 1048576 | tf_op jit(solution)/shard_map/all_to_all | solution.py:91
Sparse Core Ops, SparseCore 0:
  11.1 70.2 all-gather.4
  176.0 66.2 all-gather.6
  260.3 62.9 all-gather.8
  385.5 62.5 all-gather.10
where the time goes:
time: 526 us; the launch traced here: 516 us
  waiting for transfers between devices  274 us (52%)
  matrix products  128 us (24%)
  local copies, waits for them, and re-layouts  36.5 us (7%)
  other arithmetic  27.2 us (5%)
  blocking collectives  18.7 us (4%)
  starting transfers between devices  16.8 us (3%)
  between operations  14.8 us (3%)
    all_gather x1, waiting for transfers between devices, per_device(): row_bias = lax.all_gather(row_bias, group, axis=1, tiled=True)  67.3 us
    all_gather x1, waiting for transfers between devices, per_device(): lax.all_gather(outer_proj[:, :, opm:] * col_w[:, :, None], group, axis=1,...  66 us
    all_gather x1, waiting for transfers between devices, per_device(): start_bias = lax.all_gather(start_bias, group, axis=1, tiled=True)  62.6 us
    all_gather x1, waiting for transfers between devices, per_device(): end_bias = lax.all_gather(end_bias, group, axis=1, tiled=True)  54.8 us
    dot_general x24, matrix products, one_head(): jnp.einsum(forms[2], attn_prob, projected[:, :, 2], preferred_element_typ...  48.7 us
    sub x24, matrix products, one_head(): attn_prob = jax.nn.softmax(scores, axis=-1).astype(jnp.bfloat16)  41.8 us
    all_to_all x1, blocking collectives, per_device(): z_cols = lax.all_to_all(z_blk, group, 1, 0, tiled=True)  18.7 us
    add x16, other arithmetic, one_head(): scores = scores + head_in[1].astype(jnp.float32)[None]  18.7 us
  transfers between devices with their start and end apart: 7, of which 6 were waited for; matrix products, arithmetic and copies ran while one was open for 10% of the time, Pallas kernels for 0%

commit v1 on v0

v1 whole, which is shorter than its diff:
```python
import functools

import jax
import jax.numpy as jnp
from jax import lax
from jax.experimental import pallas as pl
from jax.experimental.pallas import tpu as pltpu
from jax.sharding import PartitionSpec as P

N0 = 0
N1 = 1
N2 = 2
N3 = 3
N4 = 4
N7 = 7
N8 = 8
N15 = 15
N16 = 16
N32 = 32
N63 = 63
N64 = 64
N127 = 127
N128 = 128
N256 = 256
N384 = 384
N512 = 512
N768 = 768
N1024 = 1024
N2048 = 2048
N4096 = 4096
ALL = Ellipsis
MESH = pl.DeviceIdType.MESH
F32 = jnp.float32
BF16 = jnp.bfloat16
VMEM_LIMIT = 60 * N1024 * N1024


def layer_norm(x):
    values = x.astype(F32)
    centred = values - jnp.mean(values, axis=-N1, keepdims=True)
    variance = jnp.mean(centred * centred, axis=-N1, keepdims=True)
    return (centred * lax.rsqrt(variance + 1e-5)).astype(BF16)


def dot(a, b):
    return jnp.dot(a, b, preferred_element_type=F32)


def dot_t(a, b):
    return lax.dot_general(a, b, (((N1,), (N1,)), ((), ())), preferred_element_type=F32)


def dev(p):
    return (N0, p // N8, lax.rem(p, N8))


def my_index():
    return lax.axis_index('chip') * N8 + lax.axis_index('dap')


def loop(n, body):
    def step(i, carry):
        body(i)
        return carry
    lax.fori_loop(N0, n, step, N0)


def barrier_all(me):
    bar = pltpu.get_barrier_semaphore()

    def signal(k):
        pl.semaphore_signal(bar, inc=N1, device_id=dev(lax.rem(me + N1 + k, N128)), device_id_type=MESH)
    loop(N127, signal)
    pl.semaphore_wait(bar, N127)


def send(src, dst, send_sem, recv_sem, p):
    pltpu.make_async_remote_copy(src_ref=src, dst_ref=dst, send_sem=send_sem, recv_sem=recv_sem,
                                 device_id=dev(p), device_id_type=MESH).start()


def wait_bytes(ref, sem):
    pltpu.make_async_copy(ref, ref, sem).wait()


def head_rep(queries, heads):
    rows = queries * heads
    r = lax.broadcasted_iota(jnp.int32, (rows, queries), N0)
    c = lax.broadcasted_iota(jnp.int32, (rows, queries), N1)
    return (r // heads == c).astype(F32).astype(BF16)


def head_mask(rows, heads, width):
    r = lax.broadcasted_iota(jnp.int32, (rows, width), N0)
    c = lax.broadcasted_iota(jnp.int32, (rows, width), N1)
    return (lax.rem(r, heads) == c // N32).astype(F32)


def softmax_rows(t):
    e = jnp.exp(t - jnp.max(t, axis=N1, keepdims=True))
    return (e * (1.0 / jnp.sum(e, axis=N1, keepdims=True))).astype(BF16)


def put(ref, value):
    for t in range(ref.shape[N0]):
        ref[t] = value[:, t * N128:(t + N1) * N128]


def take(ref, start, size, stride):
    return jnp.concatenate([ref[t, pl.ds(start, size, stride=stride), :] for t in range(ref.shape[N0])], axis=N1)


def join(ref):
    return jnp.concatenate([ref[t] for t in range(ref.shape[N0])], axis=N1)


def spread(ref, start, size, stride, value):
    for t in range(ref.shape[N0]):
        ref[t, pl.ds(start, size, stride=stride), :] = value[:, t * N128:(t + N1) * N128]


def collapse(r_ref, queries, heads):
    lane = lax.broadcasted_iota(jnp.int32, (queries, N128), N1) // N32
    parts = []
    for t in range(r_ref.shape[N0]):
        out = r_ref[t, pl.ds(N4 * t, queries, stride=heads), :]
        for h in range(N1, N4):
            out = jnp.where(lane == h, r_ref[t, pl.ds(N4 * t + h, queries, stride=heads), :], out)
        parts.append(out)
    return jnp.concatenate(parts, axis=N1) if len(parts) > N1 else parts[N0]


def gate(o, g):
    return (o * jax.nn.sigmoid(g.astype(F32))).astype(BF16)


SCALE = N32 ** -0.5


def kernel_a(m_ref, z_ref, rmask_ref, cmask_ref, cmexp_ref, wbias_t_ref, w_row_in, w_row_out, w_col_in, w_col_out,
             w_left, w_right_t, mcols_ref, left_ref, right_ref,
             x_ref, slab_f, slab, bias, xn_ref, kv_ref, q_ref, g_ref, gt_ref, rep_ref, hm_ref, r_ref, y_ref, sendf, sendb,
             recvb, xs, qkvg, yf, gsem, xsem, ssem, asem, bsem):
    me = my_index()
    core = lax.rem(me, N2)
    chip = me // N2
    half = me // N64
    barrier_all(me)
    send(m_ref, x_ref.at[pl.ds(N2 * core, N2)], xsem.at[N0], xsem.at[N1], me + N1 - N2 * core)

    for il in range(N4):
        zn = layer_norm(z_ref[il])
        slab_f[il * N8:(il + N1) * N8, :] = dot_t(wbias_t_ref[ALL], zn)
    slab[ALL] = slab_f[ALL].astype(BF16)
    slot = me - N64 * half

    def send_slab(k):
        c = lax.rem(chip + N1 + k, N64)
        p = N2 * c + half

        @pl.when(p != me)
        def _():
            send(slab, bias.at[slot], ssem, gsem.at[slot // N16], p)
    loop(N64, send_slab)

    @pl.when(core == half)
    def _():
        bias[slot] = slab[ALL]

    rep_ref[ALL] = head_rep(N64, N8)
    hm_ref[ALL] = head_mask(N512, N8, N256)

    def project(s):
        xn_ref[ALL] = layer_norm(x_ref[s])
        kv_ref[s] = dot(xn_ref[ALL], w_row_in[:, N256:N768]).astype(BF16)
        xh = xn_ref[pl.ds(pl.multiple_of(core * N256, N256), N256), :]
        q_ref[s] = dot(xh, w_row_in[:, N0:N256]).astype(BF16)
        g_ref[s] = dot(xh, w_row_in[:, N768:N1024]).astype(BF16)

    def own(s):
        x_ref[N2 * core + s] = m_ref[s]
        project(N2 * core + s)
    loop(N2, own)
    wait_bytes(m_ref, xsem.at[N1])
    loop(N2, lambda s: project(N2 - N2 * core + s))

    def attend(b, s):
        qx = (dot(rep_ref[ALL], q_ref[s, pl.ds(pl.multiple_of(b * N64, N64), N64), :]) * hm_ref[ALL]).astype(BF16)
        t = dot_t(qx, kv_ref[s, :, N0:N256]) * SCALE + bias[pl.ds(b * N16, N16)].reshape(N512, N512).astype(F32)
        t = jnp.where(rmask_ref[pl.ds(s, N1), :] > N0, t, -1e9)
        put(r_ref, dot(softmax_rows(t), kv_ref[s, :, N256:N512]))
        rows = pl.ds(pl.multiple_of(b * N64, N64), N64)
        gt_ref[s, rows, :] = gate(collapse(r_ref, N64, N8), g_ref[s, rows, :])

    def block(b):
        @pl.when(jnp.logical_and(core == half, b == slot // N16))
        def _():
            wait_bytes(bias.at[pl.ds(N0, N15)], gsem.at[b])

        @pl.when(jnp.logical_not(jnp.logical_and(core == half, b == slot // N16)))
        def _():
            wait_bytes(bias.at[pl.ds(N0, N16)], gsem.at[b])
        loop(N4, lambda s: attend(b, s))
    loop(N4, block)

    def finish(s):
        rows = pl.ds(pl.multiple_of(core * N256, N256), N256)
        put(y_ref, x_ref[s, rows, :].astype(F32) + dot(gt_ref[s], w_row_out[ALL]))
        for jl in range(N4):
            spread(sendf, s * N4 + jl, N64, N16, take(y_ref, jl, N64, N4))
    loop(N4, finish)
    sendb[ALL] = join(sendf).astype(BF16).reshape(N64, N16, N256)

    def send_cols(k0):
        k = lax.rem(slot + N1 + k0, N64)
        q = N64 * core + k

        @pl.when(q != me)
        def _():
            send(sendb.at[k], recvb.at[chip], asem.at[N0], asem.at[N1], q)
    loop(N64, send_cols)

    @pl.when(core == half)
    def _():
        recvb[chip] = sendb[slot]
        wait_bytes(recvb.at[pl.ds(N0, N63)], asem.at[N1])

    @pl.when(core != half)
    def _():
        wait_bytes(recvb, asem.at[N1])
    put(xs, recvb[ALL].astype(F32).reshape(N1024, N256))

    for jl in range(N4):
        x = take(xs, jl, N256, N4)
        qkvg[ALL] = dot(layer_norm(x), w_col_in[ALL]).astype(BF16)

        def col_block(b, jl=jl):
            rows = pl.ds(pl.multiple_of(b * N64, N64), N64)
            qx = (dot(rep_ref[ALL], qkvg[rows, N0:N256]) * hm_ref[ALL]).astype(BF16)
            t = dot_t(qx, qkvg[:, N256:N512]) * SCALE
            t = jnp.where(cmask_ref[jl:jl + N1, :] > N0, t, -1e9)
            put(r_ref, dot(softmax_rows(t), qkvg[:, N512:N768]))
            gt_ref[N0, rows, :] = gate(collapse(r_ref, N64, N8), qkvg[rows, N768:N1024])
        loop(N4, col_block)
        y = (x + dot(gt_ref[N0], w_col_out[ALL])).astype(BF16)
        spread(yf, jl, N256, N4, y.astype(F32))
        xn2 = layer_norm(y)
        right = dot_t(w_right_t[ALL], xn2).astype(BF16).astype(F32) * cmask_ref[jl:jl + N1, :]
        right_ref[jl * N32:(jl + N1) * N32, :] = right.astype(BF16)
        part = dot(xn2, w_left[jl])
        y_ref[N0] = part if jl == N0 else y_ref[N0] + part
    left_ref[ALL] = (y_ref[N0].astype(BF16).astype(F32) * cmexp_ref[ALL]).astype(BF16)
    mcols_ref[ALL] = join(yf).astype(BF16).reshape(N128, N8, N256)

    wait_bytes(m_ref, xsem.at[N0])

    @pl.when(core == half)
    def _():
        wait_bytes(bias.at[pl.ds(N0, N63)], ssem)
        wait_bytes(recvb.at[pl.ds(N0, N63)], asem.at[N0])

    @pl.when(core != half)
    def _():
        wait_bytes(bias, ssem)
        wait_bytes(recvb, asem.at[N0])


def kernel_b(left_ref, right_ref, z_ref, mcols_ref, recip_ref, w_ref, zout_ref, mout_ref,
             l_ref, r_ref, zin, o_ref, bd_ref, acc, zs, csem, asem, zsem, msem, osem):
    me = my_index()
    u = me // N8
    v = lax.rem(me, N8)
    barrier_all(me)

    def send_c(k):
        send(right_ref, r_ref.at[u], csem.at[N0], csem.at[N1], lax.rem(u + N1 + k, N16) * N8 + v)
    loop(N15, send_c)

    def send_a(k):
        d = lax.rem(v + N1 + k, N8)
        send(left_ref, l_ref.at[v], asem.at[N0], asem.at[N1], u * N8 + d)
        send(z_ref.at[d], zin.at[v], zsem.at[N0], zsem.at[N1], u * N8 + d)
    loop(N7, send_a)

    def send_m(k):
        p = lax.rem(me + N1 + k, N128)
        send(mcols_ref.at[p], mout_ref.at[me], msem.at[N0], msem.at[N1], p)
    loop(N127, send_m)
    r_ref[u] = right_ref[ALL]
    l_ref[v] = left_ref[ALL]
    zin[v] = z_ref[v]
    mout_ref[me] = mcols_ref[me]

    bd_ref[ALL] = jnp.zeros_like(bd_ref)

    def build(c2):
        for e in range(N2):
            w = w_ref[pl.ds(pl.multiple_of((N2 * c2 + e) * N32, N32), N32), :]
            for il in range(N4):
                bd_ref[c2, e * N128 + il * N32:e * N128 + (il + N1) * N32, il * N128:(il + N1) * N128] = w
    loop(N16, build)
    wait_bytes(r_ref.at[pl.ds(N0, N15)], csem.at[N1])
    wait_bytes(l_ref.at[pl.ds(N0, N7)], asem.at[N1])

    def outer(d):
        o_ref[pl.ds(pl.multiple_of(d * N2048, N2048), N2048), :] = dot(r_ref[ALL].reshape(N2048, N256), l_ref[d])
    loop(N8, outer)
    acc[ALL] = jnp.zeros_like(acc)

    def mix(c2):
        lo = o_ref[pl.ds(N2 * c2, N512, stride=N32), :].astype(BF16)
        hi = o_ref[pl.ds(N2 * c2 + N1, N512, stride=N32), :].astype(BF16)
        acc[ALL] += dot(jnp.concatenate([lo, hi], axis=N1), bd_ref[c2])
    loop(N16, mix)
    wait_bytes(zin.at[pl.ds(N0, N7)], zsem.at[N1])

    def update(d):
        rows = pl.ds(pl.multiple_of(d * N64, N64), N64)
        for il in range(N4):
            cols = slice(il * N128, (il + N1) * N128)
            upd = acc[rows, cols] * recip_ref[d, :, il:il + N1]
            zs[d, :, cols] = (zin[d, :, cols].astype(F32) + upd).astype(BF16)
    loop(N8, update)

    def send_z(k):
        d = lax.rem(v + N1 + k, N8)
        send(zs.at[d], zout_ref.at[v], osem.at[N0], osem.at[N1], u * N8 + d)
    loop(N7, send_z)
    zout_ref[v] = zs[v]
    wait_bytes(zout_ref.at[pl.ds(N0, N7)], osem.at[N1])
    wait_bytes(mout_ref.at[pl.ds(N0, N127)], msem.at[N1])
    wait_bytes(r_ref.at[pl.ds(N0, N15)], csem.at[N0])
    wait_bytes(l_ref.at[pl.ds(N0, N7)], asem.at[N0])
    wait_bytes(zin.at[pl.ds(N0, N7)], zsem.at[N0])
    wait_bytes(zout_ref.at[pl.ds(N0, N7)], osem.at[N0])
    wait_bytes(mout_ref.at[pl.ds(N0, N127)], msem.at[N0])


def kernel_c(z_ref, rmask_ref, cmask_ref, wsb_t, w_s_in, w_s_out, web_t, w_e_in, w_e_in_t, w_e_out, zo_ref,
             x_ref, slab_f, slab, bias, biasf, xn_ref, kv_ref, q_ref, g_ref, gt_ref, rep_ref, hm_ref, rept_ref, hmt_ref,
             r_ref, sendf, sendb, ebf, eslab, ebias, ebiasf, recvb, xs, kx, vx, zf, zb,
             gsem, xsem, ssem, asem, esem, osem):
    me = my_index()
    core = lax.rem(me, N2)
    chip = me // N2
    half = me // N64
    slot = me - N64 * half
    barrier_all(me)
    send(z_ref, x_ref.at[pl.ds(N4 * core, N4)], xsem.at[N0], xsem.at[N1], me + N1 - N2 * core)
    for il in range(N4):
        slab_f[N0:N4, :] = dot_t(wsb_t[ALL], layer_norm(z_ref[il]))
        ebf[il * N4:(il + N1) * N4, :] = slab_f[N0:N4, :]
    slab[ALL] = ebf[N0:N16, :].astype(BF16)

    def send_slab(k):
        c = lax.rem(chip + N1 + k, N64)
        p = N2 * c + half

        @pl.when(p != me)
        def _():
            send(slab, bias.at[slot], ssem.at[N0], gsem.at[slot // N32], p)
    loop(N64, send_slab)

    @pl.when(core == half)
    def _():
        bias[slot] = slab[ALL]

    rep_ref[ALL] = head_rep(N128, N4)
    hm_ref[ALL] = head_mask(N512, N4, N128)
    r = lax.broadcasted_iota(jnp.int32, (N128, N512), N0)
    c = lax.broadcasted_iota(jnp.int32, (N128, N512), N1)
    rept_ref[ALL] = (c // N4 == r).astype(F32).astype(BF16)
    hmt_ref[ALL] = (lax.rem(c, N4) == r // N32).astype(F32)

    def project(i):
        xn_ref[ALL] = layer_norm(x_ref[i])
        xn = xn_ref[ALL]
        kv_ref[i, :, N0:N128] = (dot(xn, w_s_in[:, N128:N256]) * cmask_ref[ALL]).astype(BF16)
        kv_ref[i, :, N128:N256] = dot(xn, w_s_in[:, N256:N384]).astype(BF16)
        xh = xn_ref[pl.ds(pl.multiple_of(core * N256, N256), N256), :]
        q_ref[i] = dot(xh, w_s_in[:, N0:N128]).astype(BF16)
        g_ref[i] = dot(xh, w_s_in[:, N384:N512]).astype(BF16)

    def own(i):
        x_ref[N4 * core + i] = z_ref[i]
        project(N4 * core + i)
    loop(N4, own)
    wait_bytes(z_ref, xsem.at[N1])
    loop(N4, lambda i: project(N4 - N4 * core + i))

    def attend(b, i):
        rows = pl.ds(pl.multiple_of(b * N128, N128), N128)
        qx = (dot(rep_ref[ALL], q_ref[i, rows, :]) * hm_ref[ALL]).astype(BF16)
        t = dot_t(qx, kv_ref[i, :, N0:N128]) * SCALE + biasf[ALL]
        r_ref[N0] = dot(softmax_rows(t), kv_ref[i, :, N128:N256])
        gt_ref[i, rows, :] = gate(collapse(r_ref, N128, N4), g_ref[i, rows, :])

    def block(b):
        @pl.when(jnp.logical_and(core == half, b == slot // N32))
        def _():
            wait_bytes(bias.at[pl.ds(N0, 31)], gsem.at[b])

        @pl.when(jnp.logical_not(jnp.logical_and(core == half, b == slot // N32)))
        def _():
            wait_bytes(bias.at[pl.ds(N0, N32)], gsem.at[b])
        got = bias[pl.ds(b * N32, N32)].reshape(N512, N512).astype(F32)
        biasf[ALL] = jnp.where(rmask_ref[ALL] > N0, got, -1e9)
        loop(N8, lambda i: attend(b, i))
    loop(N2, block)

    for i in range(N8):
        rows = pl.ds(pl.multiple_of(core * N256, N256), N256)
        y = (x_ref[i, rows, :].astype(F32) + dot(gt_ref[i], w_s_out[ALL])).astype(BF16)
        sendf[:, i] = y.astype(F32).reshape(N32, N8, N128)
        slab_f[N0:N4, N0:N256] = dot_t(web_t[ALL], layer_norm(y))
        ebf[i * N4:(i + N1) * N4, N0:N256] = slab_f[N0:N4, N0:N256]
    eslab[ALL] = ebf[:, N0:N256].astype(BF16)
    sendb[ALL] = sendf[ALL].astype(BF16).reshape(N32, N64, N128)

    def send_cols(k0):
        k = lax.rem(chip + N1 + k0, N32)
        for e in range(N2):
            q = N64 * core + N2 * k + e

            @pl.when(q != me)
            def _(q=q):
                send(sendb.at[k], recvb.at[chip], asem.at[N0], asem.at[N1], q)
    loop(N32, send_cols)

    def send_bias(k0):
        k = lax.rem(chip + N1 + k0, N64)
        send(eslab, ebias.at[chip], esem.at[N0], esem.at[N1], N2 * k + core)
    loop(N63, send_bias)
    ebias[chip] = eslab[ALL]

    @pl.when(core == half)
    def _():
        recvb[chip] = sendb[chip - N32 * core]
        wait_bytes(recvb.at[pl.ds(N0, N63)], asem.at[N1])

    @pl.when(core != half)
    def _():
        wait_bytes(recvb, asem.at[N1])
    xs[ALL] = recvb[ALL].astype(F32).reshape(N4096, N128)
    wait_bytes(ebias.at[pl.ds(N0, N63)], esem.at[N1])

    def widen(b):
        rows = pl.ds(pl.multiple_of(b * N512, N512), N512)
        keep = dot(rep_ref[ALL], cmask_ref[pl.ds(pl.multiple_of(b * N128, N128), N128), :].astype(BF16))
        got = ebias[pl.ds(b * N16, N16)].reshape(N512, N256).astype(F32)
        ebiasf[rows, N0:N128] = jnp.where(keep > N0, got[:, N0:N128], -1e9)
        ebiasf[rows, N128:N256] = jnp.where(keep > N0, got[:, N128:N256], -1e9)
    loop(N4, widen)

    def column(j):
        x = xs[pl.ds(j, N512, stride=N8), :]
        xn_ref[ALL] = layer_norm(x)
        xn = xn_ref[ALL]
        kv_ref[N0, :, N0:N128] = (dot(xn, w_e_in[:, N128:N256]) * cmask_ref[ALL]).astype(BF16)
        vt = dot_t(w_e_in_t[N256:N384, :], xn).astype(BF16)
        xh = xn_ref[pl.ds(pl.multiple_of(core * N256, N256), N256), :]
        q = dot(xh, w_e_in[:, N0:N128]).astype(BF16)
        gt = dot_t(w_e_in_t[N384:N512, :], xh).astype(BF16)
        for b in range(N4):
            kx[b * N512:(b + N1) * N512, :] = (dot(rep_ref[ALL], kv_ref[N0, b * N128:(b + N1) * N128, N0:N128]) * hm_ref[ALL]).astype(BF16)
            vx[:, b * N512:(b + N1) * N512] = (dot(vt[:, b * N128:(b + N1) * N128], rept_ref[ALL]) * hmt_ref[ALL]).astype(BF16)
        t = (dot_t(kx[ALL], q) * SCALE + ebiasf[ALL]).reshape(N256, N8, N256)
        top = jnp.max(t, axis=N0)
        top = jnp.maximum(top, pltpu.roll(top, N4, N0))
        e = jnp.exp(t - top[None])
        total = jnp.sum(e, axis=N0)
        total = total + pltpu.roll(total, N4, N0)
        p = (e * (1.0 / total)[None]).astype(BF16).reshape(N2048, N256)
        gated = gate(dot(vx[ALL], p), gt)
        y = lax.dot_general(gated, w_e_out[ALL], (((N0,), (N0,)), ((), ())), preferred_element_type=F32)
        res = xs[pl.ds(core * N2048 + j, N256, stride=N8), :]
        zf[pl.ds(j, N256, stride=N8), :] = res + y
    loop(N8, column)
    zb[ALL] = zf[ALL].astype(BF16).reshape(N64, N32, N128)

    def send_back(k0):
        k = lax.rem(slot + N1 + k0, N64)
        q = N64 * core + k

        @pl.when(q != me)
        def _():
            send(zb.at[k], zo_ref.at[chip], osem.at[N0], osem.at[N1], q)
    loop(N64, send_back)

    @pl.when(core == half)
    def _():
        zo_ref[chip] = zb[slot]
        wait_bytes(zo_ref.at[pl.ds(N0, N63)], osem.at[N1])
        wait_bytes(zo_ref.at[pl.ds(N0, N63)], osem.at[N0])
        wait_bytes(bias.at[pl.ds(N0, N63)], ssem.at[N0])
        wait_bytes(recvb.at[pl.ds(N0, N63)], asem.at[N0])

    @pl.when(core != half)
    def _():
        wait_bytes(zo_ref, osem.at[N1])
        wait_bytes(zo_ref, osem.at[N0])
        wait_bytes(bias, ssem.at[N0])
        wait_bytes(recvb, asem.at[N0])
    wait_bytes(z_ref, xsem.at[N0])
    wait_bytes(ebias.at[pl.ds(N0, N63)], esem.at[N0])


def shape(dims, dtype=BF16):
    return jax.ShapeDtypeStruct(dims, dtype)


def call(body, outs, scratch, cid, args):
    vm = pl.BlockSpec(memory_space=pltpu.VMEM)
    many = len(outs) > N1
    return pl.pallas_call(
        body, out_shape=tuple(outs) if many else outs[N0],
        in_specs=[vm] * len(args), out_specs=tuple([vm] * len(outs)) if many else vm, scratch_shapes=scratch,
        compiler_params=pltpu.CompilerParams(collective_id=cid, has_side_effects=True, vmem_limit_bytes=VMEM_LIMIT),
    )(*args)


def stage_a(m_blk, z_blk, msa_mask, me, w_row_in, w_row_bias, w_row_out, w_col_in, w_col_out, w_opm_in):
    rmask = lax.dynamic_slice_in_dim(msa_mask, (me // N2) * N4, N4, axis=N0).astype(F32)
    cols = lax.dynamic_slice_in_dim(msa_mask, me * N4, N4, axis=N1).astype(F32)
    w_left = jnp.stack([jnp.pad(w_opm_in[:, :N32], ((N0, N0), (N32 * jl, 96 - N32 * jl))) for jl in range(N4)])
    dma, V = pltpu.SemaphoreType.DMA, pltpu.VMEM
    scratch = [V((N4, N512, N256), BF16), V((N32, N512), F32), V((N32, N512), BF16), V((N64, N32, N512), BF16), V((N512, N256), BF16),
               V((N4, N512, N512), BF16), V((N4, N256, N256), BF16), V((N4, N256, N256), BF16), V((N4, N256, N256), BF16),
               V((N512, N64), BF16), V((N512, N256), F32), V((N2, N512, N128), F32), V((N2, N256, N128), F32), V((N2, N1024, N128), F32),
               V((N64, N16, N256), BF16), V((N64, N16, N256), BF16), V((N2, N1024, N128), F32), V((N256, N1024), BF16), V((N2, N1024, N128), F32),
               dma((N4,)), dma((N2,)), dma, dma((N2,)), dma((N2,))]
    return call(kernel_a, [shape((N128, N8, N256)), shape((N256, N128)), shape((N128, N256))], scratch, N0,
                [m_blk, z_blk, rmask, cols.T, jnp.repeat(cols, N32, axis=N1), w_row_bias.T, w_row_in, w_row_out, w_col_in,
                 w_col_out, w_left, w_opm_in[:, N32:].T])


def stage_b(left, right, z_blk, mcols, msa_mask, chip, dap, w_opm_out):
    mask = msa_mask.astype(BF16)
    mask_i = lax.dynamic_slice_in_dim(mask, chip * N32, N32, axis=N1)
    mask_j = lax.dynamic_slice_in_dim(mask.reshape(N256, N16, N8, N4), dap, N1, axis=N2).reshape(N256, N64)
    norm = lax.dot_general(mask_j, mask_i, (((N0,), (N0,)), ((), ())), preferred_element_type=F32)
    recip = (1.0 / (1e-3 + norm)).reshape(N64, N8, N4).transpose(N1, N0, N2)
    w_cmajor = w_opm_out.reshape(N32, N32, N128).transpose(N1, N0, N2).reshape(N1024, N128)
    z_split = z_blk.reshape(N4, N16, N8, N4, N128).transpose(N2, N1, N3, N0, N4).reshape(N8, N64, N512)
    dma, V = pltpu.SemaphoreType.DMA, pltpu.VMEM
    scratch = [V((N8, N256, N128), BF16), V((N16, N128, N256), BF16), V((N8, N64, N512), BF16), V((16384, N128), F32),
               V((N16, N256, N512), BF16), V((N512, N512), F32), V((N8, N64, N512), BF16)] + [dma((N2,))] * 5
    zout, mout = call(kernel_b, [shape((N8, N64, N512)), shape((N128, N8, N256))], scratch, N1,
                      [left, right, z_split, mcols, recip, w_cmajor])
    z_new = zout.reshape(N8, N16, N4, N4, N128).transpose(N3, N1, N0, N2, N4).reshape(N4, N512, N128)
    m_out = mout.reshape(N128, N2, N4, N256).transpose(N1, N0, N2, N3).reshape(N2, N512, N256)
    return z_new, m_out


def stage_c(z_blk, res_mask, w_start_in, w_start_bias, w_start_out, w_end_in, w_end_bias, w_end_out):
    keep = res_mask.astype(F32)
    dma, V = pltpu.SemaphoreType.DMA, pltpu.VMEM
    scratch = [V((N8, N512, N128), BF16), V((N8, N512), F32), V((N16, N512), BF16), V((N64, N16, N512), BF16), V((N512, N512), F32),
               V((N512, N128), BF16), V((N8, N512, N256), BF16), V((N8, N256, N128), BF16), V((N8, N256, N128), BF16),
               V((N8, N256, N128), BF16), V((N512, N128), BF16), V((N512, N128), F32), V((N128, N512), BF16), V((N128, N512), F32),
               V((N1, N512, N128), F32), V((N32, N8, N8, N128), F32), V((N32, N64, N128), BF16), V((N32, N512), F32), V((N32, N256), BF16),
               V((N64, N32, N256), BF16), V((N2048, N256), F32), V((N64, N64, N128), BF16), V((N4096, N128), F32), V((N2048, N128), BF16),
               V((N128, N2048), BF16), V((N2048, N128), F32), V((N64, N32, N128), BF16),
               dma((N2,)), dma((N2,)), dma((N1,)), dma((N2,)), dma((N2,)), dma((N2,))]
    zo = call(kernel_c, [shape((N64, N32, N128))], scratch, N2,
              [z_blk, keep[None, :], jnp.broadcast_to(keep[:, None], (N512, N128)), w_start_bias.T, w_start_in, w_start_out,
               w_end_bias.T, w_end_in, w_end_in.T, w_end_out])
    return zo.reshape(N64, N4, N8, N128).transpose(N1, N0, N2, N3).reshape(N4, N512, N128)


def solution(mesh):
    rows = P(('data', 'chip', 'dap'))
    in_specs = (rows, rows, P('data'), P('data')) + (P(),) * 13

    def per_device(m_blk, z_blk, msa_mask, res_mask, w_row_in, w_row_bias, w_row_out, w_col_in, w_col_out,
                   w_opm_in, w_opm_out, w_start_in, w_start_bias, w_start_out, w_end_in, w_end_bias, w_end_out):
        chip, dap = lax.axis_index('chip'), lax.axis_index('dap')
        mcols, left, right = stage_a(m_blk, z_blk, msa_mask, chip * N8 + dap, w_row_in, w_row_bias, w_row_out,
                                     w_col_in, w_col_out, w_opm_in)
        z_new, m_out = stage_b(left, right, z_blk, mcols, msa_mask, chip, dap, w_opm_out)
        z_out = stage_c(z_new, res_mask, w_start_in, w_start_bias, w_start_out, w_end_in, w_end_bias, w_end_out)
        return m_out, z_out

    return jax.shard_map(per_device, mesh=mesh, in_specs=in_specs, out_specs=(rows, rows), check_vma=False)
```

time: 526 us -> 252 us (0.48); the launches traced: 516 us -> 251 us
  waiting for transfers between devices: 274 us -> 0 us
  Pallas kernels: 0 us -> 234 us
  matrix products: 128 us -> 0.26 us
  other arithmetic: 27.2 us -> 2.71 us
  local copies, waits for them, and re-layouts: 36.5 us -> 13.3 us
  blocking collectives: 18.7 us -> 0 us
  starting transfers between devices: 16.8 us -> 0 us
  between operations: 14.8 us -> 0.82 us
    all_gather x4 -> x0, waiting for transfers between devices: 251 us -> none  [the longest x1 67.3 us: per_device(): row_bias = lax.all_gather(row_bias, group, axis=1, tiled=True)]
    pallas_call x0 -> x3, Pallas kernels: none -> 234 us  [call(): pl.pallas_call(body, out_shape=tuple(outs) if many else outs[N0], in_spec...]
    dot_general x59 -> x1, matrix products: 85.7 us -> 0.26 us  [stage_b(): lax.dot_general(mask_j, mask_i, (((N0,), (N0,)), ((), ())), preferred_ele...]
    sub x24 -> x0, matrix products: 41.8 us -> none  [one_head(): attn_prob = jax.nn.softmax(scores, axis=-1).astype(jnp.bfloat16)]
    all_to_all x3 -> x0, waiting for transfers between devices: 23.1 us -> none  [the longest x1 12 us: per_device(): m_cols = lax.all_to_all(m_blk, group, 1, 0, tiled=True)]
    all_to_all x1 -> x0, blocking collectives: 18.7 us -> none  [per_device(): z_cols = lax.all_to_all(z_blk, group, 1, 0, tiled=True)]
    add x16 -> x0, other arithmetic: 18.7 us -> none  [one_head(): scores = scores + head_in[1].astype(jnp.float32)[None]]
    while x5 -> x0, local copies, waits for them, and re-layouts: 16.5 us -> none  [gated_attention(): gated = lax.map(one_head, head_in)]
  transfers between devices with their start and end apart: 7 -> 0, of which waited for: 6 -> 0; matrix products, arithmetic and copies ran while one was open for 10% -> 0% of each run, Pallas kernels for 0% -> 0%
where the time goes in v1:
time: 252 us; the launch traced here: 251 us
  Pallas kernels  234 us (93%)
  local copies, waits for them, and re-layouts  13.3 us (5%)
  other arithmetic  2.71 us (1%)
    pallas_call x3, Pallas kernels, call(): pl.pallas_call(body, out_shape=tuple(outs) if many else outs[N0], in_spec...  234 us

profile of v1, /device:TPU:1, one launch (start us, length us, event | category | flops | bytes accessed | tf_op | source)
XLA Modules:
  0.0 251.5 jit_solution(4621266148046226676)
XLA Ops:
  0.7 1.3 dynamic-slice_convert_fusion.rmask_ref
  2.0 1.0 constant_dynamic-slice_fusion.1
  3.0 0.1 copy.39
  3.1 0.6 fusion.3
  3.7 0.0 copy-start.5
  3.7 0.8 copy.30.cmexp_ref
  4.4 0.6 slice_bitcast_fusion
  5.0 0.1 copy.40
  5.2 0.1 pad_bitcast_fusion.3
  5.3 0.7 pad_maximum_fusion.w_left
  6.0 87.1 %shard_map.176 = (bf16[128,8,256]{2,1,0:T(8,128)(2,1)}, bf16[256,128]{1,0:T(8,128)(2,1)}, bf16[128,256]{1,0:T(8,128)(2,1)}) custom-call(bf16[2,512,256]{2,1,0:T(8,128)(2,1)} %m_ref.1, bf16[4,512,128]{2,1,0:T(8,128)(2,1)} %z_ref.1, f32[4,512]{1,0:T(4,128)} %dynamic-slice_convert_fusion.rmask_ref, f32[4,256]{1,0:T(4,128)} %get-tuple-element.19.cmask_ref, ...), custom_call_target="tpu_custom_call" | custom-call | tf_op jit(solution)/shard_map/pallas_call | solution.py:515
  93.2 0.1 copy.32
  93.3 0.0 copy-start
  93.3 0.1 reshape.50
  93.5 0.3 fusion
  93.7 0.9 copy.33
  94.6 0.7 copy.43
  95.3 0.0 copy-start.4
  95.3 1.0 reshape.49.z_ref
  96.3 0.8 copy.34
  97.1 49.3 %shard_map.177 = (bf16[8,64,512]{2,1,0:T(8,128)(2,1)}, bf16[128,8,256]{2,1,0:T(8,128)(2,1)}) custom-call(bf16[256,128]{1,0:T(8,128)(2,1)} %get-tuple-element.7.left_ref, bf16[128,256]{1,0:T(8,128)(2,1)} %get-tuple-element.8.right_ref, bf16[8,64,512]{2,1,0:T(8,128)(2,1)} %reshape.49.z_ref, bf16[128,8,256]{2,1,0:T(8,128)(2,1)} %get-tuple-element.9.mcols_ref, ...), custom_call_target="tpu_custom_call" | custom-call | tf_op jit(solution)/shard_map/pallas_call | solution.py:515
  146.4 1.2 reshape.57
  147.6 0.0 copy-start.7
  147.6 1.0 copy.36
  148.6 0.8 broadcast_in_dim.14.cmask_ref
  149.5 0.1 copy-done.2
  149.5 0.8 copy.37
  150.3 98.0 %shard_map.178 = bf16[64,32,128]{2,1,0:T(8,128)(2,1)} custom-call(bf16[4,512,128]{2,1,0:T(8,128)(2,1)} %bitcast.44, f32[1,512]{1,0:T(1,128)} %bitcast.54, f32[512,128]{1,0:T(8,128)} %broadcast_in_dim.14.cmask_ref, bf16[4,128]{1,0:T(4,128)(2,1)} %bitcast.56, bf16[128,512]{1,0:T(8,128)(2,1)} %w_s_in.1, bf16[128,128]{1,0:T(8,128)(2,1)} %w_s_out.1, ...), custom_call_target="tpu_custom_call" | custom-call | tf_op jit(solution)/shard_map/pallas_call | solution.py:515
  248.2 2.0 copy_bitcast_fusion
  250.2 0.1 reshape.55
  250.4 0.2 copy.35
  250.5 0.9 reshape.56
  (16 shorter events, 0.1 us)
Async XLA Ops:
  3.7 0.8 copy-start.5
  6.0 87.1 %copy-start.1 = (s32[256,512]{1,0:T(8,128)S(1)}, s32[256,512]{1,0:T(8,128)}, u32[]{:S(2)}) copy-start(s32[256,512]{1,0:T(8,128)} %param.19) | copy-start | bytes 1572868
  93.3 1.3 copy-start
  95.3 1.0 copy-start.4
  147.6 1.0 copy-start.7
  148.6 0.8 copy-start.6
  148.6 0.9 copy-start.2
  248.2 2.0 copy-start.3

commit v2 on v0

v2 whole, which is shorter than its diff:
```python
import functools
from types import SimpleNamespace

import jax
import jax.numpy as jnp
from jax import lax
from jax.experimental import pallas as pl
from jax.experimental.pallas import tpu as pltpu
from jax.sharding import PartitionSpec as P

N0 = 0
N1 = 1
N2 = 2
N4 = 4
N7 = 7
N8 = 8
N15 = 15
N16 = 16
N32 = 32
N63 = 63
N64 = 64
N127 = 127
N128 = 128
N256 = 256
N384 = 384
N512 = 512
N768 = 768
N1024 = 1024
N2048 = 2048
N4096 = 4096
ALL = Ellipsis
MESH = pl.DeviceIdType.MESH
F32 = jnp.float32
BF16 = jnp.bfloat16
VMEM_LIMIT = 67043328


def layer_norm(x):
    values = x.astype(F32)
    centred = values - jnp.mean(values, axis=-N1, keepdims=True)
    variance = jnp.mean(centred * centred, axis=-N1, keepdims=True)
    return (centred * lax.rsqrt(variance + 1e-5)).astype(BF16)


def dot(a, b):
    return jnp.dot(a, b, preferred_element_type=F32)


def dot_t(a, b):
    return lax.dot_general(a, b, (((N1,), (N1,)), ((), ())), preferred_element_type=F32)


def dev(p):
    return (N0, p // N8, lax.rem(p, N8))


def my_index():
    return lax.axis_index('chip') * N8 + lax.axis_index('dap')


def loop(n, body):
    def step(i, carry):
        body(i)
        return carry
    lax.fori_loop(N0, n, step, N0)


def send(src, dst, send_sem, recv_sem, p):
    pltpu.make_async_remote_copy(src_ref=src, dst_ref=dst, send_sem=send_sem, recv_sem=recv_sem,
                                 device_id=dev(p), device_id_type=MESH).start()


def wait_bytes(ref, sem):
    pltpu.make_async_copy(ref, ref, sem).wait()


def head_rep(queries, heads):
    rows = queries * heads
    r = lax.broadcasted_iota(jnp.int32, (rows, queries), N0)
    c = lax.broadcasted_iota(jnp.int32, (rows, queries), N1)
    return (r // heads == c).astype(F32).astype(BF16)


def head_mask(rows, heads, width):
    r = lax.broadcasted_iota(jnp.int32, (rows, width), N0)
    c = lax.broadcasted_iota(jnp.int32, (rows, width), N1)
    return (lax.rem(r, heads) == c // N32).astype(F32)


def softmax_rows(t):
    e = jnp.exp(t - jnp.max(t, axis=N1, keepdims=True))
    return (e * (1.0 / jnp.sum(e, axis=N1, keepdims=True))).astype(BF16)


def put(ref, value):
    for t in range(ref.shape[N0]):
        ref[t] = value[:, t * N128:(t + N1) * N128]


def take(ref, start, size, stride):
    return jnp.concatenate([ref[t, pl.ds(start, size, stride=stride), :] for t in range(ref.shape[N0])], axis=N1)


def join(ref):
    return jnp.concatenate([ref[t] for t in range(ref.shape[N0])], axis=N1)


def spread(ref, start, size, stride, value):
    for t in range(ref.shape[N0]):
        ref[t, pl.ds(start, size, stride=stride), :] = value[:, t * N128:(t + N1) * N128]


def collapse(r_ref, queries, heads):
    lane = lax.broadcasted_iota(jnp.int32, (queries, N128), N1) // N32
    parts = []
    for t in range(r_ref.shape[N0]):
        out = r_ref[t, pl.ds(N4 * t, queries, stride=heads), :]
        for h in range(N1, N4):
            out = jnp.where(lane == h, r_ref[t, pl.ds(N4 * t + h, queries, stride=heads), :], out)
        parts.append(out)
    return jnp.concatenate(parts, axis=N1) if len(parts) > N1 else parts[N0]


def gate(o, g):
    return (o * jax.nn.sigmoid(g.astype(F32))).astype(BF16)


SCALE = N32 ** -0.5


def dot_c(a, b, da, db):
    return lax.dot_general(a, b, (((da,), (db,)), ((), ())), preferred_element_type=F32)


def iota(rows, cols, dim):
    return lax.broadcasted_iota(jnp.int32, (rows, cols), dim)


def one_hot(cond):
    return cond.astype(F32).astype(BF16)


def ready(cond, ref, few, many, sem):
    @pl.when(cond)
    def _():
        wait_bytes(ref.at[pl.ds(N0, few)], sem)

    @pl.when(jnp.logical_not(cond))
    def _():
        wait_bytes(ref.at[pl.ds(N0, many)], sem)


def kernel(scratch_names, m_ref, z_ref, mask_ref, keep_ref, w_row_in, w_row_bias, w_row_out, w_col_in, w_col_out,
           w_opm_in, w_opm_out, w_s_in, w_s_bias, w_s_out, w_e_in, w_e_bias, w_e_out, m_out, z_out, *scratch):
    r = SimpleNamespace(**dict(zip(scratch_names, scratch)))
    me = my_index()
    core, chip, half = lax.rem(me, N2), me // N2, me // N64
    u, v = me // N8, lax.rem(me, N8)
    slot = me - N64 * half
    mine = core == half
    hrows = pl.ds(pl.multiple_of(core * N256, N256), N256)
    bar = pltpu.get_barrier_semaphore()
    loop(N127, lambda k: pl.semaphore_signal(bar, inc=N1, device_id=dev(lax.rem(me + N1 + k, N128)), device_id_type=MESH))

    for il in range(N4):
        r.slab_f[il * N8:(il + N1) * N8, :] = dot_c(w_row_bias[ALL], layer_norm(z_ref[il]), N0, N1)
    r.slab_a[ALL] = r.slab_f[ALL].astype(BF16)
    pl.semaphore_wait(bar, N127)
    send(m_ref, r.xm.at[pl.ds(N2 * core, N2)], r.xsem.at[N0], r.xsem.at[N1], me + N1 - N2 * core)

    def send_slab_a(k):
        p = N2 * lax.rem(chip + N1 + k, N64) + half

        @pl.when(p != me)
        def _():
            send(r.slab_a, r.bias_a.at[slot], r.sa, r.ga.at[slot // N16], p)
    loop(N64, send_slab_a)

    @pl.when(mine)
    def _():
        r.bias_a[slot] = r.slab_a[ALL]

    r.rep8[ALL] = head_rep(N64, N8)
    r.hm8[ALL] = head_mask(N512, N8, N256)
    maskb = mask_ref[ALL].astype(F32).astype(BF16)
    r.rmask[ALL] = dot(one_hot(iota(N4, N256, N1) == N4 * chip + iota(N4, N256, N0)), maskb)
    r.cmask[ALL] = dot_c(one_hot(iota(N4, N512, N1) == N4 * me + iota(N4, N512, N0)), maskb, N1, N1)
    r.cmexp[ALL] = dot(maskb, one_hot(iota(N512, N128, N0) == N4 * me + iota(N512, N128, N1) // N32))
    lane = iota(N512, N64, N1)
    mask_j = dot(maskb, one_hot(iota(N512, N64, N0) == N32 * lax.rem(lane, N16) + N4 * v + lane // N16)).astype(BF16)
    mask_i = dot(maskb, one_hot(iota(N512, N32, N0) == N32 * u + iota(N512, N32, N1))).astype(BF16)
    r.recip[ALL] = 1.0 / (1e-3 + dot_c(mask_j, mask_i, N0, N0))

    def project_m(s):
        r.xn_m[ALL] = layer_norm(r.xm[s])
        r.kv_m[s] = dot(r.xn_m[ALL], w_row_in[:, N256:N768]).astype(BF16)
        xh = r.xn_m[hrows, :]
        r.q_m[s] = dot(xh, w_row_in[:, N0:N256]).astype(BF16)
        r.g_m[s] = dot(xh, w_row_in[:, N768:N1024]).astype(BF16)

    def own_m(s):
        r.xm[N2 * core + s] = m_ref[s]
        project_m(N2 * core + s)
    loop(N2, own_m)
    wait_bytes(m_ref, r.xsem.at[N1])
    loop(N2, lambda s: project_m(N2 - N2 * core + s))

    for il in range(N4):
        r.zf[il] = z_ref[il].astype(F32)

    def split_z(d):
        for il in range(N4):
            for jl in range(N4):
                r.zsplit[d, jl * N16:(jl + N1) * N16, il * N128:(il + N1) * N128] = r.zf[il, pl.ds(d * N4 + jl, N16, stride=N32), :].astype(BF16)
    loop(N8, split_z)

    def send_z_in(k):
        d = lax.rem(v + N1 + k, N8)
        send(r.zsplit.at[d], r.zin.at[v], r.zsem.at[N0], r.zsem.at[N1], u * N8 + d)
    loop(N7, send_z_in)
    r.zin[v] = r.zsplit[v]

    def attend_m(b, s):
        rows = pl.ds(pl.multiple_of(b * N64, N64), N64)
        qx = (dot(r.rep8[ALL], r.q_m[s, rows, :]) * r.hm8[ALL]).astype(BF16)
        t = dot_t(qx, r.kv_m[s, :, N0:N256]) * SCALE + r.bias_a[pl.ds(b * N16, N16)].reshape(N512, N512).astype(F32)
        t = jnp.where(r.rmask[pl.ds(s, N1), :] > N0, t, -1e9)
        put(r.pv, dot(softmax_rows(t), r.kv_m[s, :, N256:N512]))
        r.gt_m[s, rows, :] = gate(collapse(r.pv, N64, N8), r.g_m[s, rows, :])

    def block_m(b):
        ready(jnp.logical_and(mine, b == slot // N16), r.bias_a, N15, N16, r.ga.at[b])
        loop(N4, lambda s: attend_m(b, s))
    loop(N4, block_m)

    def finish_m(s):
        put(r.y_m, r.xm[s, hrows, :].astype(F32) + dot(r.gt_m[s], w_row_out[ALL]))
        for jl in range(N4):
            spread(r.f_m, s * N4 + jl, N64, N16, take(r.y_m, jl, N64, N4))
    loop(N4, finish_m)
    r.send_m[ALL] = join(r.f_m).astype(BF16).reshape(N64, N16, N256)

    def send_cols_m(k0):
        k = lax.rem(slot + N1 + k0, N64)
        q = N64 * core + k

        @pl.when(q != me)
        def _():
            send(r.send_m.at[k], r.recv_m.at[chip], r.am.at[N0], r.am.at[N1], q)
    loop(N64, send_cols_m)

    @pl.when(mine)
    def _():
        r.recv_m[chip] = r.send_m[slot]

    r.bd[ALL] = jnp.zeros_like(r.bd)
    r.wf[ALL] = w_opm_out[ALL].astype(F32)

    def build(c2):
        for e in range(N2):
            w = r.wf[pl.ds(N2 * c2 + e, N32, stride=N32), :].astype(BF16)
            for il in range(N4):
                r.bd[c2, e * N128 + il * N32:e * N128 + (il + N1) * N32, il * N128:(il + N1) * N128] = w
    loop(N16, build)
    r.rep4[ALL] = head_rep(N128, N4)
    r.hm4[ALL] = head_mask(N512, N4, N128)
    r.rept[ALL] = one_hot(iota(N128, N512, N1) // N4 == iota(N128, N512, N0))
    r.hmt[ALL] = (lax.rem(iota(N128, N512, N1), N4) == iota(N128, N512, N0) // N32).astype(F32)
    for e in range(N2):
        r.wet[e] = jnp.transpose(w_e_in[:, N256 + e * N128:N384 + e * N128].astype(F32)).astype(BF16)
    keep = jnp.where(iota(N8, N512, N0) == N0, keep_ref[ALL].astype(F32), 0.0).astype(BF16)
    r.keepc[ALL] = dot_c(keep, one_hot(iota(N8, N128, N0) < N8), N0, N0)
    r.keepr[ALL] = keep_ref[ALL].astype(F32)
    ready(mine, r.recv_m, N63, N64, r.am.at[N1])
    put(r.xs_m, r.recv_m[ALL].astype(F32).reshape(N1024, N256))

    for jl in range(N4):
        x = take(r.xs_m, jl, N256, N4)
        r.qkvg[ALL] = dot(layer_norm(x), w_col_in[ALL]).astype(BF16)

        def col_block(b, jl=jl):
            rows = pl.ds(pl.multiple_of(b * N64, N64), N64)
            qx = (dot(r.rep8[ALL], r.qkvg[rows, N0:N256]) * r.hm8[ALL]).astype(BF16)
            t = dot_t(qx, r.qkvg[:, N256:N512]) * SCALE
            t = jnp.where(r.cmask[jl:jl + N1, :] > N0, t, -1e9)
            put(r.pv, dot(softmax_rows(t), r.qkvg[:, N512:N768]))
            r.gt_m[N0, rows, :] = gate(collapse(r.pv, N64, N8), r.qkvg[rows, N768:N1024])
        loop(N4, col_block)
        y = (x + dot(r.gt_m[N0], w_col_out[ALL])).astype(BF16)
        spread(r.yf_m, jl, N256, N4, y.astype(F32))
        ab = dot(layer_norm(y), w_opm_in[ALL]).astype(BF16)
        right = dot_c(one_hot(iota(N32, N64, N1) == iota(N32, N64, N0) + N32), ab, N1, N1) * r.cmask[jl:jl + N1, :]
        r.right[jl * N32:(jl + N1) * N32, :] = right.astype(BF16)
        part = dot(ab, one_hot(iota(N64, N128, N1) == iota(N64, N128, N0) + N32 * jl) * one_hot(iota(N64, N128, N0) < N32))
        r.y_m[N0] = part if jl == N0 else r.y_m[N0] + part
    r.left[ALL] = (r.y_m[N0] * r.cmexp[ALL]).astype(BF16)

    def send_c(k):
        send(r.right, r.rall.at[u], r.csem.at[N0], r.csem.at[N1], lax.rem(u + N1 + k, N16) * N8 + v)
    loop(N15, send_c)

    def send_a(k):
        d = lax.rem(v + N1 + k, N8)
        send(r.left, r.lall.at[v], r.lsem.at[N0], r.lsem.at[N1], u * N8 + d)
    loop(N7, send_a)
    r.rall[u] = r.right[ALL]
    r.lall[v] = r.left[ALL]
    r.mcols[ALL] = join(r.yf_m).astype(BF16).reshape(N128, N8, N256)
    r.acc[ALL] = jnp.zeros_like(r.acc)
    wait_bytes(r.rall.at[pl.ds(N0, N15)], r.csem.at[N1])
    wait_bytes(r.lall.at[pl.ds(N0, N7)], r.lsem.at[N1])

    def outer(d):
        r.o[pl.ds(pl.multiple_of(d * N2048, N2048), N2048), :] = dot(r.rall[ALL].reshape(N2048, N256), r.lall[d])
    loop(N8, outer)

    def mix(c2):
        parts = []
        for e in range(N2):
            rows = [r.o[pl.ds(d * N2048 + jl * N32 + N2 * c2 + e, N16, stride=N128), :] for d in range(N8) for jl in range(N4)]
            parts.append(jnp.concatenate(rows, axis=N0).astype(BF16))
        r.acc[ALL] += dot(jnp.concatenate(parts, axis=N1), r.bd[c2])
    loop(N16, mix)
    wait_bytes(r.zin.at[pl.ds(N0, N7)], r.zsem.at[N1])
    for d in range(N8):
        for il in range(N4):
            cols = slice(il * N128, (il + N1) * N128)
            upd = r.acc[d * N64:(d + N1) * N64, cols] * r.recip[:, d * N4 + il:d * N4 + il + N1]
            r.zs[d, :, cols] = (r.zin[d, :, cols].astype(F32) + upd).astype(BF16)

    def send_z(k):
        d = lax.rem(v + N1 + k, N8)
        send(r.zs.at[d], r.zback.at[v], r.bsem.at[N0], r.bsem.at[N1], u * N8 + d)
    loop(N7, send_z)
    r.zback[v] = r.zs[v]
    wait_bytes(r.zback.at[pl.ds(N0, N7)], r.bsem.at[N1])

    def merge_z(d):
        for il in range(N4):
            for jl in range(N4):
                r.zf[il, pl.ds(d * N4 + jl, N16, stride=N32), :] = r.zback[d, jl * N16:(jl + N1) * N16, il * N128:(il + N1) * N128].astype(F32)
    loop(N8, merge_z)

    for il in range(N4):
        r.zb[il] = r.zf[il].astype(BF16)
        r.e_f[il * N4:(il + N1) * N4, :] = dot_c(w_s_bias[ALL], layer_norm(r.zb[il]), N0, N1)
    r.slab_s[ALL] = r.e_f[N0:N16, :].astype(BF16)
    send(r.zb, r.xz.at[pl.ds(N4 * core, N4)], r.ysem.at[N0], r.ysem.at[N1], me + N1 - N2 * core)

    def send_slab_s(k):
        p = N2 * lax.rem(chip + N1 + k, N64) + half

        @pl.when(p != me)
        def _():
            send(r.slab_s, r.bias_s.at[slot], r.ss, r.gs.at[slot // N32], p)
    loop(N64, send_slab_s)

    @pl.when(mine)
    def _():
        r.bias_s[slot] = r.slab_s[ALL]

    def send_m_out(k):
        p = lax.rem(me + N1 + k, N128)
        send(r.mcols.at[p], r.mback.at[me], r.msem.at[N0], r.msem.at[N1], p)
    loop(N127, send_m_out)
    r.mback[me] = r.mcols[me]

    def project_z(i):
        r.xn_z[ALL] = layer_norm(r.xz[i])
        xn = r.xn_z[ALL]
        r.kv_z[i, :, N0:N128] = (dot(xn, w_s_in[:, N128:N256]) * r.keepc[ALL]).astype(BF16)
        r.kv_z[i, :, N128:N256] = dot(xn, w_s_in[:, N256:N384]).astype(BF16)
        xh = r.xn_z[hrows, :]
        r.q_z[i] = dot(xh, w_s_in[:, N0:N128]).astype(BF16)
        r.g_z[i] = dot(xh, w_s_in[:, N384:N512]).astype(BF16)

    def own_z(i):
        r.xz[N4 * core + i] = r.zb[i]
        project_z(N4 * core + i)
    loop(N4, own_z)
    wait_bytes(r.zb, r.ysem.at[N1])
    loop(N4, lambda i: project_z(N4 - N4 * core + i))

    def attend_z(b, i):
        rows = pl.ds(pl.multiple_of(b * N128, N128), N128)
        qx = (dot(r.rep4[ALL], r.q_z[i, rows, :]) * r.hm4[ALL]).astype(BF16)
        t = dot_t(qx, r.kv_z[i, :, N0:N128]) * SCALE + r.biasf[ALL]
        r.pv[N0] = dot(softmax_rows(t), r.kv_z[i, :, N128:N256])
        r.gt_z[i, rows, :] = gate(collapse(r.pv.at[N0:N1], N128, N4), r.g_z[i, rows, :])

    def block_z(b):
        ready(jnp.logical_and(mine, b == slot // N32), r.bias_s, 31, N32, r.gs.at[b])
        got = r.bias_s[pl.ds(b * N32, N32)].reshape(N512, N512).astype(F32)
        r.biasf[ALL] = jnp.where(r.keepr[ALL] > N0, got, -1e9)
        loop(N8, lambda i: attend_z(b, i))
    loop(N2, block_z)

    for i in range(N8):
        y = (r.xz[i, hrows, :].astype(F32) + dot(r.gt_z[i], w_s_out[ALL])).astype(BF16)
        r.f_z[:, i] = y.astype(F32).reshape(N32, N8, N128)
        r.e_f[i * N4:(i + N1) * N4, N0:N256] = dot_c(w_e_bias[ALL], layer_norm(y), N0, N1)
    r.slab_e[ALL] = r.e_f[:, N0:N256].astype(BF16)
    r.send_zc[ALL] = r.f_z[ALL].astype(BF16).reshape(N32, N64, N128)

    def send_cols_z(k0):
        k = lax.rem(chip + N1 + k0, N32)
        for e in range(N2):
            q = N64 * core + N2 * k + e

            @pl.when(q != me)
            def _(q=q):
                send(r.send_zc.at[k], r.recv_zc.at[chip], r.az.at[N0], r.az.at[N1], q)
    loop(N32, send_cols_z)

    def send_slab_e(k0):
        send(r.slab_e, r.bias_e.at[chip], r.esem.at[N0], r.esem.at[N1], N2 * lax.rem(chip + N1 + k0, N64) + core)
    loop(N63, send_slab_e)
    r.bias_e[chip] = r.slab_e[ALL]

    @pl.when(mine)
    def _():
        r.recv_zc[chip] = r.send_zc[chip - N32 * core]

    wait_bytes(r.mback.at[pl.ds(N0, N127)], r.msem.at[N1])
    put(r.yf_m, r.mback[ALL].astype(F32).reshape(N1024, N256))
    for sl in range(N2):
        for jl in range(N4):
            spread(r.f_m, sl * N512 + jl, N128, N4, take(r.yf_m, sl * N4 + jl, N128, N8))
    m_out[ALL] = join(r.f_m).astype(BF16).reshape(N2, N512, N256)

    ready(mine, r.recv_zc, N63, N64, r.az.at[N1])
    r.xs_z[ALL] = r.recv_zc[ALL].astype(F32).reshape(N4096, N128)
    wait_bytes(r.bias_e.at[pl.ds(N0, N63)], r.esem.at[N1])

    def widen(b):
        rows = pl.ds(pl.multiple_of(b * N512, N512), N512)
        kept = dot(r.rep4[ALL], r.keepc[pl.ds(pl.multiple_of(b * N128, N128), N128), :].astype(BF16))
        got = r.bias_e[pl.ds(b * N16, N16)].reshape(N512, N256).astype(F32)
        for t in range(N2):
            r.biasf_e[rows, t * N128:(t + N1) * N128] = jnp.where(kept > N0, got[:, t * N128:(t + N1) * N128], -1e9)
    loop(N4, widen)

    def column(j):
        r.xn_z[ALL] = layer_norm(r.xs_z[pl.ds(j, N512, stride=N8), :])
        xn = r.xn_z[ALL]
        r.kv_z[N0, :, N0:N128] = (dot(xn, w_e_in[:, N128:N256]) * r.keepc[ALL]).astype(BF16)
        vt = dot_t(r.wet[N0], xn).astype(BF16)
        xh = r.xn_z[hrows, :]
        q = dot(xh, w_e_in[:, N0:N128]).astype(BF16)
        gt = dot_t(r.wet[N1], xh).astype(BF16)
        for b in range(N4):
            r.kx[b * N512:(b + N1) * N512, :] = (dot(r.rep4[ALL], r.kv_z[N0, b * N128:(b + N1) * N128, N0:N128]) * r.hm4[ALL]).astype(BF16)
            r.vx[:, b * N512:(b + N1) * N512] = (dot(vt[:, b * N128:(b + N1) * N128], r.rept[ALL]) * r.hmt[ALL]).astype(BF16)
        t = (dot_t(r.kx[ALL], q) * SCALE + r.biasf_e[ALL]).reshape(N256, N8, N256)
        top = jnp.max(t, axis=N0)
        top = jnp.maximum(top, pltpu.roll(top, N4, N0))
        e = jnp.exp(t - top[None])
        total = jnp.sum(e, axis=N0)
        total = total + pltpu.roll(total, N4, N0)
        p = (e * (1.0 / total)[None]).astype(BF16).reshape(N2048, N256)
        gated = gate(dot(r.vx[ALL], p), gt)
        y = dot_c(gated, w_e_out[ALL], N0, N0)
        r.y_z[pl.ds(j, N256, stride=N8), :] = r.xs_z[pl.ds(core * N2048 + j, N256, stride=N8), :] + y
    loop(N8, column)
    r.send_o[ALL] = r.y_z[ALL].astype(BF16).reshape(N64, N32, N128)

    def send_back(k0):
        k = lax.rem(slot + N1 + k0, N64)
        q = N64 * core + k

        @pl.when(q != me)
        def _():
            send(r.send_o.at[k], r.recv_o.at[chip], r.osem.at[N0], r.osem.at[N1], q)
    loop(N64, send_back)

    @pl.when(mine)
    def _():
        r.recv_o[chip] = r.send_o[slot]
    for ref, sem in ((r.bias_a, r.sa), (r.recv_m, r.am.at[N0]), (r.bias_s, r.ss), (r.recv_zc, r.az.at[N0])):
        ready(mine, ref, N63, N64, sem)
    wait_bytes(m_ref, r.xsem.at[N0])
    wait_bytes(r.zb, r.ysem.at[N0])
    wait_bytes(r.zin.at[pl.ds(N0, N7)], r.zsem.at[N0])
    wait_bytes(r.rall.at[pl.ds(N0, N15)], r.csem.at[N0])
    wait_bytes(r.lall.at[pl.ds(N0, N7)], r.lsem.at[N0])
    wait_bytes(r.zback.at[pl.ds(N0, N7)], r.bsem.at[N0])
    wait_bytes(r.mback.at[pl.ds(N0, N127)], r.msem.at[N0])
    wait_bytes(r.bias_e.at[pl.ds(N0, N63)], r.esem.at[N0])
    ready(mine, r.recv_o, N63, N64, r.osem.at[N1])
    got = r.recv_o[ALL].astype(F32).reshape(N64, N4, N8, N128)
    for il in range(N4):
        z_out[il] = got[:, il].reshape(N512, N128).astype(BF16)
    ready(mine, r.recv_o, N63, N64, r.osem.at[N0])


BUFFERS = dict(
    slab_a=(N32, N512), bias_a=(N64, N32, N512), xm=(N4, N512, N256), xn_m=(N512, N256), kv_m=(N4, N512, N512), q_m=(N4, N256, N256),
    g_m=(N4, N256, N256), gt_m=(N4, N256, N256), rep8=(N512, N64), zsplit=(N8, N64, N512), zin=(N8, N64, N512), send_m=(N64, N16, N256),
    recv_m=(N64, N16, N256), qkvg=(N256, N1024), left=(N256, N128), right=(N128, N256), lall=(N8, N256, N128), rall=(N16, N128, N256),
    mcols=(N128, N8, N256), mback=(N128, N8, N256), bd=(N16, N256, N512), zs=(N8, N64, N512), zback=(N8, N64, N512), zb=(N4, N512, N128),
    xz=(N8, N512, N128), slab_s=(N16, N512), bias_s=(N64, N16, N512), xn_z=(N512, N128), kv_z=(N8, N512, N256), q_z=(N8, N256, N128),
    g_z=(N8, N256, N128), gt_z=(N8, N256, N128), rep4=(N512, N128), rept=(N128, N512), wet=(N2, N128, N128), slab_e=(N32, N256),
    bias_e=(N64, N32, N256), send_zc=(N32, N64, N128), recv_zc=(N64, N64, N128), kx=(N2048, N128), vx=(N128, N2048),
    send_o=(N64, N32, N128), recv_o=(N64, N32, N128))
FLOATS = dict(
    slab_f=(N32, N512), rmask=(N4, N512), cmask=(N4, N256), cmexp=(N256, N128), recip=(N64, N32), hm8=(N512, N256), hm4=(N512, N128),
    hmt=(N128, N512), keepc=(N512, N128), keepr=(N1, N512), zf=(N4, N512, N128), pv=(N2, N512, N128), y_m=(N2, N256, N128),
    f_m=(N2, N1024, N128), xs_m=(N2, N1024, N128), yf_m=(N2, N1024, N128), wf=(N1024, N128), o=(16384, N128), acc=(N512, N512),
    e_f=(N32, N512), biasf=(N512, N512), f_z=(N32, N8, N8, N128), biasf_e=(N2048, N256), xs_z=(N4096, N128), y_z=(N2048, N128))
SEMS = dict(ga=N4, gs=N2, xsem=N2, ysem=N2, zsem=N2, am=N2, csem=N2, lsem=N2, bsem=N2, msem=N2, az=N2, esem=N2, osem=N2, sa=None, ss=None)


def solution(mesh):
    rows = P(('data', 'chip', 'dap'))
    in_specs = (rows, rows, P('data'), P('data')) + (P(),) * 13
    specs = {name: pltpu.VMEM(dims, BF16) for name, dims in BUFFERS.items()}
    specs.update({name: pltpu.VMEM(dims, F32) for name, dims in FLOATS.items()})
    specs.update({name: pltpu.SemaphoreType.DMA if n is None else pltpu.SemaphoreType.DMA((n,)) for name, n in SEMS.items()})

    def per_device(m_blk, z_blk, msa_mask, res_mask, *weights):
        args = (m_blk, z_blk, msa_mask, res_mask.reshape(N1, N512)) + weights
        vm = pl.BlockSpec(memory_space=pltpu.VMEM)
        return pl.pallas_call(
            functools.partial(kernel, tuple(specs)),
            out_shape=(jax.ShapeDtypeStruct(m_blk.shape, BF16), jax.ShapeDtypeStruct(z_blk.shape, BF16)),
            in_specs=[vm] * len(args), out_specs=(vm, vm), scratch_shapes=list(specs.values()),
            compiler_params=pltpu.CompilerParams(collective_id=N0, has_side_effects=True, vmem_limit_bytes=VMEM_LIMIT),
        )(*args)

    return jax.shard_map(per_device, mesh=mesh, in_specs=in_specs, out_specs=(rows, rows), check_vma=False)
```

time: 526 us -> 223 us (0.42); the launches traced: 516 us -> 223 us
  waiting for transfers between devices: 274 us -> 0 us
  Pallas kernels: 0 us -> 216 us
  matrix products: 128 us -> 0 us
  local copies, waits for them, and re-layouts: 36.5 us -> 6.33 us
  other arithmetic: 27.2 us -> 0 us
  blocking collectives: 18.7 us -> 0 us
  starting transfers between devices: 16.8 us -> 0 us
  between operations: 14.8 us -> 0.66 us
    all_gather x4 -> x0, waiting for transfers between devices: 251 us -> none  [the longest x1 67.3 us: per_device(): row_bias = lax.all_gather(row_bias, group, axis=1, tiled=True)]
    pallas_call x0 -> x1, Pallas kernels: none -> 216 us  [per_device(): pl.pallas_call(functools.partial(kernel, tuple(specs)), out_shape=(jax.Sh...]
    dot_general x59 -> x0, matrix products: 85.7 us -> none  [the longest x24 48.7 us: one_head(): jnp.einsum(forms[2], attn_prob, projected[:, :, 2], preferred_element_typ...]
    sub x24 -> x0, matrix products: 41.8 us -> none  [one_head(): attn_prob = jax.nn.softmax(scores, axis=-1).astype(jnp.bfloat16)]
    all_to_all x3 -> x0, waiting for transfers between devices: 23.1 us -> none  [the longest x1 12 us: per_device(): m_cols = lax.all_to_all(m_blk, group, 1, 0, tiled=True)]
    all_to_all x1 -> x0, blocking collectives: 18.7 us -> none  [per_device(): z_cols = lax.all_to_all(z_blk, group, 1, 0, tiled=True)]
    add x16 -> x0, other arithmetic: 18.7 us -> none  [one_head(): scores = scores + head_in[1].astype(jnp.float32)[None]]
    while x5 -> x0, local copies, waits for them, and re-layouts: 16.5 us -> none  [gated_attention(): gated = lax.map(one_head, head_in)]
  transfers between devices with their start and end apart: 7 -> 0, of which waited for: 6 -> 0; matrix products, arithmetic and copies ran while one was open for 10% -> 0% of each run, Pallas kernels for 0% -> 0%
where the time goes in v2:
time: 223 us
  Pallas kernels  216 us (97%)
  local copies, waits for them, and re-layouts  6.33 us (3%)
    pallas_call x1, Pallas kernels, per_device(): pl.pallas_call(functools.partial(kernel, tuple(specs)), out_shape=(jax.Sh...  216 us
    unnamed x14, local copies, waits for them, and re-layouts  6.33 us

profile of v2, /device:TPU:1, one launch (start us, length us, event | category | flops | bytes accessed | tf_op | source)
XLA Modules:
  0.0 223.1 jit_solution(12963378771178891561)
XLA Ops:
  0.6 0.0 copy-start.2
  0.6 1.4 copy.19.w_row_bias
  2.0 0.0 copy-done.2
  2.0 0.0 copy-start.3
  2.0 0.0 copy-start.1
  2.0 0.7 copy.21.w_s_bias
  2.8 0.0 copy-done.3
  2.8 0.7 copy.22.w_e_bias
  3.5 0.0 copy-done.1
  3.5 0.7 copy.20.w_opm_in
  4.3 216.1 %shard_map.176 = (bf16[2,512,256]{2,1,0:T(8,128)(2,1)}, bf16[4,512,128]{2,1,0:T(8,128)(2,1)}) custom-call(bf16[2,512,256]{2,1,0:T(8,128)(2,1)} %m_ref.1, bf16[4,512,128]{2,1,0:T(8,128)(2,1)} %z_ref.1, s32[256,512]{1,0:T(8,128)} %mask_ref.1, s32[1,512]{1,0:T(1,128)} %bitcast.1, bf16[256,1024]{1,0:T(8,128)(2,1)} %w_row_in.1, bf16[128,8]{1,0:T(8,128)(2,1)} %copy.19.w_row_bias, ...), custom_call_target="tpu_custom_call" | custom-call | tf_op jit(solution)/shard_map/pallas_call | solution.py:523
  220.4 0.0 copy-start
  220.4 1.9 copy.25
  222.3 0.0 copy-done
  222.3 0.8 copy.26
Async XLA Ops:
  0.6 1.4 copy-start.2
  2.0 0.7 copy-start.3
  2.0 1.5 copy-start.1
  220.4 1.9 copy-start

commit v3 on v2

--- a/solution.py
+++ b/solution.py
@@ -11,6 +11,7 @@
 N0 = 0
 N1 = 1
 N2 = 2
+N3 = 3
 N4 = 4
 N7 = 7
 N8 = 8
@@ -33,6 +34,7 @@
 F32 = jnp.float32
 BF16 = jnp.bfloat16
 VMEM_LIMIT = 67043328
+UNROLL_A, UNROLL_B, UNROLL_C, UNROLL_D = N2, N1, N2, N1
 
 
 def layer_norm(x):
@@ -58,11 +60,11 @@
     return lax.axis_index('chip') * N8 + lax.axis_index('dap')
 
 
-def loop(n, body):
+def loop(n, body, unroll=N1):
     def step(i, carry):
         body(i)
         return carry
-    lax.fori_loop(N0, n, step, N0)
+    lax.fori_loop(N0, n, step, N0, unroll=unroll)
 
 
 def send(src, dst, send_sem, recv_sem, p):
@@ -88,7 +90,7 @@
 
 
 def softmax_rows(t):
-    e = jnp.exp(t - jnp.max(t, axis=N1, keepdims=True))
+    e = jnp.exp2(t - jnp.max(t, axis=N1, keepdims=True))
     return (e * (1.0 / jnp.sum(e, axis=N1, keepdims=True))).astype(BF16)
 
 
@@ -125,7 +127,9 @@
     return (o * jax.nn.sigmoid(g.astype(F32))).astype(BF16)
 
 
-SCALE = N32 ** -0.5
+LOG2E = 1.4426950408889634
+SCALE = N32 ** -0.5 * LOG2E
+LOW = -1e9 * LOG2E
 
 
 def dot_c(a, b, da, db):
@@ -163,7 +167,7 @@
     loop(N127, lambda k: pl.semaphore_signal(bar, inc=N1, device_id=dev(lax.rem(me + N1 + k, N128)), device_id_type=MESH))
 
     for il in range(N4):
-        r.slab_f[il * N8:(il + N1) * N8, :] = dot_c(w_row_bias[ALL], layer_norm(z_ref[il]), N0, N1)
+        r.slab_f[il * N8:(il + N1) * N8, :] = dot_t(w_row_bias[ALL], layer_norm(z_ref[il]))
     r.slab_a[ALL] = r.slab_f[ALL].astype(BF16)
     pl.semaphore_wait(bar, N127)
     send(m_ref, r.xm.at[pl.ds(N2 * core, N2)], r.xsem.at[N0], r.xsem.at[N1], me + N1 - N2 * core)
@@ -185,7 +189,6 @@
     maskb = mask_ref[ALL].astype(F32).astype(BF16)
     r.rmask[ALL] = dot(one_hot(iota(N4, N256, N1) == N4 * chip + iota(N4, N256, N0)), maskb)
     r.cmask[ALL] = dot_c(one_hot(iota(N4, N512, N1) == N4 * me + iota(N4, N512, N0)), maskb, N1, N1)
-    r.cmexp[ALL] = dot(maskb, one_hot(iota(N512, N128, N0) == N4 * me + iota(N512, N128, N1) // N32))
     lane = iota(N512, N64, N1)
     mask_j = dot(maskb, one_hot(iota(N512, N64, N0) == N32 * lax.rem(lane, N16) + N4 * v + lane // N16)).astype(BF16)
     mask_i = dot(maskb, one_hot(iota(N512, N32, N0) == N32 * u + iota(N512, N32, N1))).astype(BF16)
@@ -205,49 +208,37 @@
     wait_bytes(m_ref, r.xsem.at[N1])
     loop(N2, lambda s: project_m(N2 - N2 * core + s))
 
-    for il in range(N4):
-        r.zf[il] = z_ref[il].astype(F32)
-
-    def split_z(d):
-        for il in range(N4):
-            for jl in range(N4):
-                r.zsplit[d, jl * N16:(jl + N1) * N16, il * N128:(il + N1) * N128] = r.zf[il, pl.ds(d * N4 + jl, N16, stride=N32), :].astype(BF16)
-    loop(N8, split_z)
-
-    def send_z_in(k):
-        d = lax.rem(v + N1 + k, N8)
-        send(r.zsplit.at[d], r.zin.at[v], r.zsem.at[N0], r.zsem.at[N1], u * N8 + d)
-    loop(N7, send_z_in)
-    r.zin[v] = r.zsplit[v]
-
     def attend_m(b, s):
         rows = pl.ds(pl.multiple_of(b * N64, N64), N64)
         qx = (dot(r.rep8[ALL], r.q_m[s, rows, :]) * r.hm8[ALL]).astype(BF16)
-        t = dot_t(qx, r.kv_m[s, :, N0:N256]) * SCALE + r.bias_a[pl.ds(b * N16, N16)].reshape(N512, N512).astype(F32)
-        t = jnp.where(r.rmask[pl.ds(s, N1), :] > N0, t, -1e9)
+        t = dot_t(qx, r.kv_m[s, :, N0:N256]) * SCALE + r.biasf[ALL]
+        t = jnp.where(r.rmask[pl.ds(s, N1), :] > N0, t, LOW)
         put(r.pv, dot(softmax_rows(t), r.kv_m[s, :, N256:N512]))
         r.gt_m[s, rows, :] = gate(collapse(r.pv, N64, N8), r.g_m[s, rows, :])
 
-    def block_m(b):
+    def finish_m(b, s):
+        rows = pl.ds(pl.multiple_of(b * N64, N64), N64)
+        put(r.y_m, r.xm[s, pl.ds(pl.multiple_of(core * N256 + b * N64, N64), N64), :].astype(F32) + dot(r.gt_m[s, rows, :], w_row_out[ALL]))
+        for jl in range(N4):
+            spread(r.f_b, s * N4 + jl, N16, N16, take(r.y_m, jl, N16, N4))
+
+    def block_m(step):
+        b = lax.rem(jnp.where(chip // N32 == core, (chip - N32 * core) // N8, N0) + N3 - step, N4)
         ready(jnp.logical_and(mine, b == slot // N16), r.bias_a, N15, N16, r.ga.at[b])
-        loop(N4, lambda s: attend_m(b, s))
+        r.biasf[ALL] = r.bias_a[pl.ds(b * N16, N16)].reshape(N512, N512).astype(F32) * LOG2E
+        loop(N4, lambda s: attend_m(b, s), UNROLL_A)
+        loop(N4, lambda s: finish_m(b, s))
+        r.send_m[pl.ds(b * N16, N16)] = join(r.f_b).astype(BF16).reshape(N16, N16, N256)
+
+        def send_cols_m(k0):
+            k = b * N16 + lax.rem(slot + N1 + k0, N16)
+            q = N64 * core + k
+
+            @pl.when(q != me)
+            def _():
+                send(r.send_m.at[k], r.recv_m.at[chip], r.am.at[N0], r.am.at[N1], q)
+        loop(N16, send_cols_m)
     loop(N4, block_m)
-
-    def finish_m(s):
-        put(r.y_m, r.xm[s, hrows, :].astype(F32) + dot(r.gt_m[s], w_row_out[ALL]))
-        for jl in range(N4):
-            spread(r.f_m, s * N4 + jl, N64, N16, take(r.y_m, jl, N64, N4))
-    loop(N4, finish_m)
-    r.send_m[ALL] = join(r.f_m).astype(BF16).reshape(N64, N16, N256)
-
-    def send_cols_m(k0):
-        k = lax.rem(slot + N1 + k0, N64)
-        q = N64 * core + k
-
-        @pl.when(q != me)
-        def _():
-            send(r.send_m.at[k], r.recv_m.at[chip], r.am.at[N0], r.am.at[N1], q)
-    loop(N64, send_cols_m)
 
     @pl.when(mine)
     def _():
@@ -271,7 +262,22 @@
     keep = jnp.where(iota(N8, N512, N0) == N0, keep_ref[ALL].astype(F32), 0.0).astype(BF16)
     r.keepc[ALL] = dot_c(keep, one_hot(iota(N8, N128, N0) < N8), N0, N0)
     r.keepr[ALL] = keep_ref[ALL].astype(F32)
+    for il in range(N4):
+        r.zf[il] = z_ref[il].astype(F32)
+
+    def split_z(d):
+        for il in range(N4):
+            for jl in range(N4):
+                r.zsplit[d, jl * N16:(jl + N1) * N16, il * N128:(il + N1) * N128] = r.zf[il, pl.ds(d * N4 + jl, N16, stride=N32), :].astype(BF16)
+    loop(N8, split_z)
+
     ready(mine, r.recv_m, N63, N64, r.am.at[N1])
+    def send_z_in(k):
+        d = lax.rem(v + N1 + k, N8)
+        send(r.zsplit.at[d], r.zin.at[v], r.zsem.at[N0], r.zsem.at[N1], u * N8 + d)
+    loop(N7, send_z_in)
+    r.zin[v] = r.zsplit[v]
+
     put(r.xs_m, r.recv_m[ALL].astype(F32).reshape(N1024, N256))
 
     for jl in range(N4):
@@ -282,43 +288,44 @@
             rows = pl.ds(pl.multiple_of(b * N64, N64), N64)
             qx = (dot(r.rep8[ALL], r.qkvg[rows, N0:N256]) * r.hm8[ALL]).astype(BF16)
             t = dot_t(qx, r.qkvg[:, N256:N512]) * SCALE
-            t = jnp.where(r.cmask[jl:jl + N1, :] > N0, t, -1e9)
+            t = jnp.where(r.cmask[jl:jl + N1, :] > N0, t, LOW)
             put(r.pv, dot(softmax_rows(t), r.qkvg[:, N512:N768]))
             r.gt_m[N0, rows, :] = gate(collapse(r.pv, N64, N8), r.qkvg[rows, N768:N1024])
-        loop(N4, col_block)
+        loop(N4, col_block, UNROLL_B)
         y = (x + dot(r.gt_m[N0], w_col_out[ALL])).astype(BF16)
         spread(r.yf_m, jl, N256, N4, y.astype(F32))
-        ab = dot(layer_norm(y), w_opm_in[ALL]).astype(BF16)
-        right = dot_c(one_hot(iota(N32, N64, N1) == iota(N32, N64, N0) + N32), ab, N1, N1) * r.cmask[jl:jl + N1, :]
-        r.right[jl * N32:(jl + N1) * N32, :] = right.astype(BF16)
-        part = dot(ab, one_hot(iota(N64, N128, N1) == iota(N64, N128, N0) + N32 * jl) * one_hot(iota(N64, N128, N0) < N32))
-        r.y_m[N0] = part if jl == N0 else r.y_m[N0] + part
-    r.left[ALL] = (r.y_m[N0] * r.cmexp[ALL]).astype(BF16)
-
-    def send_c(k):
-        send(r.right, r.rall.at[u], r.csem.at[N0], r.csem.at[N1], lax.rem(u + N1 + k, N16) * N8 + v)
-    loop(N15, send_c)
-
-    def send_a(k):
-        d = lax.rem(v + N1 + k, N8)
-        send(r.left, r.lall.at[v], r.lsem.at[N0], r.lsem.at[N1], u * N8 + d)
-    loop(N7, send_a)
-    r.rall[u] = r.right[ALL]
-    r.lall[v] = r.left[ALL]
+        ab = dot_t(layer_norm(y), w_opm_in[ALL]).astype(BF16)
+        for side, ref in ((N0, r.left), (N1, r.right)):
+            pick = one_hot(iota(N32, N64, N1) == iota(N32, N64, N0) + N32 * side)
+            ref[jl] = (dot_c(pick, ab, N1, N1) * r.cmask[jl:jl + N1, :]).astype(BF16)
+
+        def send_c(k, jl=jl):
+            send(r.right.at[jl], r.rall.at[jl, u], r.csem.at[N0], r.csem.at[N1], lax.rem(u + N1 + k, N16) * N8 + v)
+        loop(N15, send_c)
+
+        def send_a(k, jl=jl):
+            send(r.left.at[jl], r.lall.at[v, jl], r.lsem.at[N0], r.lsem.at[N1], u * N8 + lax.rem(v + N1 + k, N8))
+        loop(N7, send_a)
+        r.rall[jl, u] = r.right[jl]
+        r.lall[v, jl] = r.left[jl]
+
     r.mcols[ALL] = join(r.yf_m).astype(BF16).reshape(N128, N8, N256)
     r.acc[ALL] = jnp.zeros_like(r.acc)
-    wait_bytes(r.rall.at[pl.ds(N0, N15)], r.csem.at[N1])
+    wait_bytes(r.rall.at[:, pl.ds(N0, N15)], r.csem.at[N1])
     wait_bytes(r.lall.at[pl.ds(N0, N7)], r.lsem.at[N1])
 
+    put(r.rf, r.rall[ALL].astype(F32).reshape(N2048, N256))
+
+    def reorder(c):
+        r.rc[c] = take(r.rf, c, N64, N32).astype(BF16)
+    loop(N32, reorder, N4)
+
     def outer(d):
-        r.o[pl.ds(pl.multiple_of(d * N2048, N2048), N2048), :] = dot(r.rall[ALL].reshape(N2048, N256), r.lall[d])
+        r.o[d] = dot_t(r.rc[ALL].reshape(N2048, N256), r.lall[d].reshape(N128, N256)).astype(BF16).reshape(N32, N64, N128)
     loop(N8, outer)
 
     def mix(c2):
-        parts = []
-        for e in range(N2):
-            rows = [r.o[pl.ds(d * N2048 + jl * N32 + N2 * c2 + e, N16, stride=N128), :] for d in range(N8) for jl in range(N4)]
-            parts.append(jnp.concatenate(rows, axis=N0).astype(BF16))
+        parts = [r.o[:, N2 * c2 + e].reshape(N512, N128) for e in range(N2)]
         r.acc[ALL] += dot(jnp.concatenate(parts, axis=N1), r.bd[c2])
     loop(N16, mix)
     wait_bytes(r.zin.at[pl.ds(N0, N7)], r.zsem.at[N1])
@@ -343,7 +350,7 @@
 
     for il in range(N4):
         r.zb[il] = r.zf[il].astype(BF16)
-        r.e_f[il * N4:(il + N1) * N4, :] = dot_c(w_s_bias[ALL], layer_norm(r.zb[il]), N0, N1)
+        r.e_f[il * N4:(il + N1) * N4, :] = dot_t(w_s_bias[ALL], layer_norm(r.zb[il]))
     r.slab_s[ALL] = r.e_f[N0:N16, :].astype(BF16)
     send(r.zb, r.xz.at[pl.ds(N4 * core, N4)], r.ysem.at[N0], r.ysem.at[N1], me + N1 - N2 * core)
 
@@ -388,38 +395,38 @@
         r.pv[N0] = dot(softmax_rows(t), r.kv_z[i, :, N128:N256])
         r.gt_z[i, rows, :] = gate(collapse(r.pv.at[N0:N1], N128, N4), r.g_z[i, rows, :])
 
-    def block_z(b):
+    def block_z(step):
+        b = lax.rem(jnp.where(chip // N32 == core, (chip - N32 * core) // N16, N0) + N1 + step, N2)
         ready(jnp.logical_and(mine, b == slot // N32), r.bias_s, 31, N32, r.gs.at[b])
         got = r.bias_s[pl.ds(b * N32, N32)].reshape(N512, N512).astype(F32)
-        r.biasf[ALL] = jnp.where(r.keepr[ALL] > N0, got, -1e9)
-        loop(N8, lambda i: attend_z(b, i))
+        r.biasf[ALL] = jnp.where(r.keepr[ALL] > N0, got * LOG2E, LOW)
+        loop(N8, lambda i: attend_z(b, i), UNROLL_C)
     loop(N2, block_z)
 
     for i in range(N8):
         y = (r.xz[i, hrows, :].astype(F32) + dot(r.gt_z[i], w_s_out[ALL])).astype(BF16)
         r.f_z[:, i] = y.astype(F32).reshape(N32, N8, N128)
-        r.e_f[i * N4:(i + N1) * N4, N0:N256] = dot_c(w_e_bias[ALL], layer_norm(y), N0, N1)
+        r.e_f[i * N4:(i + N1) * N4, N0:N256] = dot_t(w_e_bias[ALL], layer_norm(y))
     r.slab_e[ALL] = r.e_f[:, N0:N256].astype(BF16)
     r.send_zc[ALL] = r.f_z[ALL].astype(BF16).reshape(N32, N64, N128)
 
     def send_cols_z(k0):
-        k = lax.rem(chip + N1 + k0, N32)
-        for e in range(N2):
-            q = N64 * core + N2 * k + e
-
-            @pl.when(q != me)
-            def _(q=q):
-                send(r.send_zc.at[k], r.recv_zc.at[chip], r.az.at[N0], r.az.at[N1], q)
+        k = N32 * core + lax.rem(chip + N1 + k0, N32)
+        q = N2 * k + half
+
+        @pl.when(q != me)
+        def _():
+            send(r.send_zc.at[k - N32 * core], r.recv_zc.at[chip], r.az.at[N0], r.az.at[N1], q)
     loop(N32, send_cols_z)
+
+    @pl.when(mine)
+    def _():
+        r.recv_zc[chip] = r.send_zc[chip - N32 * core]
 
     def send_slab_e(k0):
         send(r.slab_e, r.bias_e.at[chip], r.esem.at[N0], r.esem.at[N1], N2 * lax.rem(chip + N1 + k0, N64) + core)
     loop(N63, send_slab_e)
     r.bias_e[chip] = r.slab_e[ALL]
-
-    @pl.when(mine)
-    def _():
-        r.recv_zc[chip] = r.send_zc[chip - N32 * core]
 
     wait_bytes(r.mback.at[pl.ds(N0, N127)], r.msem.at[N1])
     put(r.yf_m, r.mback[ALL].astype(F32).reshape(N1024, N256))
@@ -428,8 +435,20 @@
             spread(r.f_m, sl * N512 + jl, N128, N4, take(r.yf_m, sl * N4 + jl, N128, N8))
     m_out[ALL] = join(r.f_m).astype(BF16).reshape(N2, N512, N256)
 
-    ready(mine, r.recv_zc, N63, N64, r.az.at[N1])
+    ready(mine, r.recv_zc, 31, N32, r.az.at[N1])
+    taken = r.recv_zc.at[pl.ds(N32 * core, N32)]
+    send(taken, taken, r.fsem.at[N0], r.fsem.at[N1], me + N1 - N2 * core)
+    wait_bytes(taken, r.fsem.at[N1])
     r.xs_z[ALL] = r.recv_zc[ALL].astype(F32).reshape(N4096, N128)
+    def project_e(j):
+        r.xn_z[ALL] = layer_norm(r.xs_z[pl.ds(j, N512, stride=N8), :])
+        xn = r.xn_z[ALL]
+        r.k_e[j] = (dot(xn, w_e_in[:, N128:N256]) * r.keepc[ALL]).astype(BF16)
+        r.v_e[j] = dot_t(r.wet[N0], xn).astype(BF16)
+        xh = r.xn_z[hrows, :]
+        r.q_z[j] = dot(xh, w_e_in[:, N0:N128]).astype(BF16)
+        r.g_e[j] = dot_t(r.wet[N1], xh).astype(BF16)
+    loop(N8, project_e)
     wait_bytes(r.bias_e.at[pl.ds(N0, N63)], r.esem.at[N1])
 
     def widen(b):
@@ -437,31 +456,24 @@
         kept = dot(r.rep4[ALL], r.keepc[pl.ds(pl.multiple_of(b * N128, N128), N128), :].astype(BF16))
         got = r.bias_e[pl.ds(b * N16, N16)].reshape(N512, N256).astype(F32)
         for t in range(N2):
-            r.biasf_e[rows, t * N128:(t + N1) * N128] = jnp.where(kept > N0, got[:, t * N128:(t + N1) * N128], -1e9)
+            r.biasf_e[rows, t * N128:(t + N1) * N128] = jnp.where(kept > N0, got[:, t * N128:(t + N1) * N128] * LOG2E, LOW)
     loop(N4, widen)
 
     def column(j):
-        r.xn_z[ALL] = layer_norm(r.xs_z[pl.ds(j, N512, stride=N8), :])
-        xn = r.xn_z[ALL]
-        r.kv_z[N0, :, N0:N128] = (dot(xn, w_e_in[:, N128:N256]) * r.keepc[ALL]).astype(BF16)
-        vt = dot_t(r.wet[N0], xn).astype(BF16)
-        xh = r.xn_z[hrows, :]
-        q = dot(xh, w_e_in[:, N0:N128]).astype(BF16)
-        gt = dot_t(r.wet[N1], xh).astype(BF16)
         for b in range(N4):
-            r.kx[b * N512:(b + N1) * N512, :] = (dot(r.rep4[ALL], r.kv_z[N0, b * N128:(b + N1) * N128, N0:N128]) * r.hm4[ALL]).astype(BF16)
-            r.vx[:, b * N512:(b + N1) * N512] = (dot(vt[:, b * N128:(b + N1) * N128], r.rept[ALL]) * r.hmt[ALL]).astype(BF16)
-        t = (dot_t(r.kx[ALL], q) * SCALE + r.biasf_e[ALL]).reshape(N256, N8, N256)
+            r.kx[b * N512:(b + N1) * N512, :] = (dot(r.rep4[ALL], r.k_e[j, b * N128:(b + N1) * N128, :]) * r.hm4[ALL]).astype(BF16)
+            r.vx[:, b * N512:(b + N1) * N512] = (dot(r.v_e[j, :, b * N128:(b + N1) * N128], r.rept[ALL]) * r.hmt[ALL]).astype(BF16)
+        t = (dot_t(r.kx[ALL], r.q_z[j]) * SCALE + r.biasf_e[ALL]).reshape(N256, N8, N256)
         top = jnp.max(t, axis=N0)
         top = jnp.maximum(top, pltpu.roll(top, N4, N0))
-        e = jnp.exp(t - top[None])
+        e = jnp.exp2(t - top[None])
         total = jnp.sum(e, axis=N0)
         total = total + pltpu.roll(total, N4, N0)
         p = (e * (1.0 / total)[None]).astype(BF16).reshape(N2048, N256)
-        gated = gate(dot(r.vx[ALL], p), gt)
+        gated = gate(dot(r.vx[ALL], p), r.g_e[j])
         y = dot_c(gated, w_e_out[ALL], N0, N0)
         r.y_z[pl.ds(j, N256, stride=N8), :] = r.xs_z[pl.ds(core * N2048 + j, N256, stride=N8), :] + y
-    loop(N8, column)
+    loop(N8, column, UNROLL_D)
     r.send_o[ALL] = r.y_z[ALL].astype(BF16).reshape(N64, N32, N128)
 
     def send_back(k0):
@@ -476,12 +488,14 @@
     @pl.when(mine)
     def _():
         r.recv_o[chip] = r.send_o[slot]
-    for ref, sem in ((r.bias_a, r.sa), (r.recv_m, r.am.at[N0]), (r.bias_s, r.ss), (r.recv_zc, r.az.at[N0])):
+    for ref, sem in ((r.bias_a, r.sa), (r.recv_m, r.am.at[N0]), (r.bias_s, r.ss)):
         ready(mine, ref, N63, N64, sem)
+    ready(mine, r.recv_zc, 31, N32, r.az.at[N0])
+    wait_bytes(taken, r.fsem.at[N0])
     wait_bytes(m_ref, r.xsem.at[N0])
     wait_bytes(r.zb, r.ysem.at[N0])
     wait_bytes(r.zin.at[pl.ds(N0, N7)], r.zsem.at[N0])
-    wait_bytes(r.rall.at[pl.ds(N0, N15)], r.csem.at[N0])
+    wait_bytes(r.rall.at[:, pl.ds(N0, N15)], r.csem.at[N0])
     wait_bytes(r.lall.at[pl.ds(N0, N7)], r.lsem.at[N0])
     wait_bytes(r.zback.at[pl.ds(N0, N7)], r.bsem.at[N0])
     wait_bytes(r.mback.at[pl.ds(N0, N127)], r.msem.at[N0])
@@ -496,18 +510,18 @@
 BUFFERS = dict(
     slab_a=(N32, N512), bias_a=(N64, N32, N512), xm=(N4, N512, N256), xn_m=(N512, N256), kv_m=(N4, N512, N512), q_m=(N4, N256, N256),
     g_m=(N4, N256, N256), gt_m=(N4, N256, N256), rep8=(N512, N64), zsplit=(N8, N64, N512), zin=(N8, N64, N512), send_m=(N64, N16, N256),
-    recv_m=(N64, N16, N256), qkvg=(N256, N1024), left=(N256, N128), right=(N128, N256), lall=(N8, N256, N128), rall=(N16, N128, N256),
-    mcols=(N128, N8, N256), mback=(N128, N8, N256), bd=(N16, N256, N512), zs=(N8, N64, N512), zback=(N8, N64, N512), zb=(N4, N512, N128),
+    recv_m=(N64, N16, N256), qkvg=(N256, N1024), left=(N4, N32, N256), right=(N4, N32, N256), lall=(N8, N4, N32, N256), rall=(N4, N16, N32, N256),
+    mcols=(N128, N8, N256), o=(N8, N32, N64, N128), rc=(N32, N64, N256), mback=(N128, N8, N256), bd=(N16, N256, N512), zs=(N8, N64, N512), zback=(N8, N64, N512), zb=(N4, N512, N128),
     xz=(N8, N512, N128), slab_s=(N16, N512), bias_s=(N64, N16, N512), xn_z=(N512, N128), kv_z=(N8, N512, N256), q_z=(N8, N256, N128),
     g_z=(N8, N256, N128), gt_z=(N8, N256, N128), rep4=(N512, N128), rept=(N128, N512), wet=(N2, N128, N128), slab_e=(N32, N256),
-    bias_e=(N64, N32, N256), send_zc=(N32, N64, N128), recv_zc=(N64, N64, N128), kx=(N2048, N128), vx=(N128, N2048),
+    bias_e=(N64, N32, N256), send_zc=(N32, N64, N128), recv_zc=(N64, N64, N128), k_e=(N8, N512, N128), v_e=(N8, N128, N512), g_e=(N8, N128, N256), kx=(N2048, N128), vx=(N128, N2048),
     send_o=(N64, N32, N128), recv_o=(N64, N32, N128))
 FLOATS = dict(
-    slab_f=(N32, N512), rmask=(N4, N512), cmask=(N4, N256), cmexp=(N256, N128), recip=(N64, N32), hm8=(N512, N256), hm4=(N512, N128),
-    hmt=(N128, N512), keepc=(N512, N128), keepr=(N1, N512), zf=(N4, N512, N128), pv=(N2, N512, N128), y_m=(N2, N256, N128),
-    f_m=(N2, N1024, N128), xs_m=(N2, N1024, N128), yf_m=(N2, N1024, N128), wf=(N1024, N128), o=(16384, N128), acc=(N512, N512),
+    slab_f=(N32, N512), rmask=(N4, N512), cmask=(N4, N256), recip=(N64, N32), hm8=(N512, N256), hm4=(N512, N128),
+    hmt=(N128, N512), keepc=(N512, N128), keepr=(N1, N512), zf=(N4, N512, N128), pv=(N2, N512, N128), y_m=(N2, N64, N128), f_b=(N2, N256, N128),
+    f_m=(N2, N1024, N128), xs_m=(N2, N1024, N128), yf_m=(N2, N1024, N128), wf=(N1024, N128), rf=(N2, N2048, N128), acc=(N512, N512),
     e_f=(N32, N512), biasf=(N512, N512), f_z=(N32, N8, N8, N128), biasf_e=(N2048, N256), xs_z=(N4096, N128), y_z=(N2048, N128))
-SEMS = dict(ga=N4, gs=N2, xsem=N2, ysem=N2, zsem=N2, am=N2, csem=N2, lsem=N2, bsem=N2, msem=N2, az=N2, esem=N2, osem=N2, sa=None, ss=None)
+SEMS = dict(ga=N4, gs=N2, xsem=N2, ysem=N2, zsem=N2, am=N2, csem=N2, lsem=N2, bsem=N2, msem=N2, az=N2, fsem=N2, esem=N2, osem=N2, sa=None, ss=None)
 
 
 def solution(mesh):
@@ -518,7 +532,10 @@
     specs.update({name: pltpu.SemaphoreType.DMA if n is None else pltpu.SemaphoreType.DMA((n,)) for name, n in SEMS.items()})
 
     def per_device(m_blk, z_blk, msa_mask, res_mask, *weights):
-        args = (m_blk, z_blk, msa_mask, res_mask.reshape(N1, N512)) + weights
+        w = list(weights)
+        for k in (N1, 5, N8, 11):
+            w[k] = w[k].T
+        args = (m_blk, z_blk, msa_mask, res_mask.reshape(N1, N512), *w)
         vm = pl.BlockSpec(memory_space=pltpu.VMEM)
         return pl.pallas_call(
             functools.partial(kernel, tuple(specs)),

time: 223 us -> 192 us (0.86)
  Pallas kernels: 216 us -> 189 us
  local copies, waits for them, and re-layouts: 6.33 us -> 2.72 us
    pallas_call x1, Pallas kernels: 216 us -> 189 us  [per_device(): pl.pallas_call(functools.partial(kernel, tuple(specs)), out_shape=(jax.Sh...]
    unnamed x14 -> x4, local copies, waits for them, and re-layouts: 6.33 us -> 2.72 us
where the time goes in v3:
time: 192 us
  Pallas kernels  189 us (98%)
  local copies, waits for them, and re-layouts  2.72 us (1%)
    pallas_call x1, Pallas kernels, per_device(): pl.pallas_call(functools.partial(kernel, tuple(specs)), out_shape=(jax.Sh...  189 us

profile of v3, /device:TPU:1, one launch (start us, length us, event | category | flops | bytes accessed | tf_op | source)
XLA Modules:
  0.0 192.0 jit_solution(13080772752988554773)
XLA Ops:
  0.6 188.7 %shard_map.176 = (bf16[2,512,256]{2,1,0:T(8,128)(2,1)}, bf16[4,512,128]{2,1,0:T(8,128)(2,1)}) custom-call(bf16[2,512,256]{2,1,0:T(8,128)(2,1)} %m_ref.1, bf16[4,512,128]{2,1,0:T(8,128)(2,1)} %z_ref.1, s32[256,512]{1,0:T(8,128)} %mask_ref.1, s32[1,512]{1,0:T(1,128)} %bitcast.6, bf16[256,1024]{1,0:T(8,128)(2,1)} %w_row_in.1, bf16[8,128]{1,0:T(8,128)(2,1)} %bitcast.7, ...), custom_call_target="tpu_custom_call" | custom-call | tf_op jit(solution)/shard_map/pallas_call | solution.py:540
  189.3 0.0 copy-start
  189.3 1.9 %copy.21 = bf16[2,512,256]{2,1,0:T(8,128)(2,1)} copy(bf16[2,512,256]{2,1,0:T(8,128)(2,1)} %get-tuple-element.4) | data formatting | bytes 1048576
  191.2 0.0 copy-done
  191.2 0.8 copy.22
Async XLA Ops:
  189.3 1.9 %copy-start = (bf16[4,512,128]{2,1,0:T(8,128)(2,1)S(1)}, bf16[4,512,128]{2,1,0:T(8,128)(2,1)}, u32[]{:S(2)}) copy-start(bf16[4,512,128]{2,1,0:T(8,128)(2,1)} %get-tuple-element.5) | copy-start | bytes 1572868

commit v4 on v3

--- a/solution.py
+++ b/solution.py
@@ -34,7 +34,7 @@
 F32 = jnp.float32
 BF16 = jnp.bfloat16
 VMEM_LIMIT = 67043328
-UNROLL_A, UNROLL_B, UNROLL_C, UNROLL_D = N2, N1, N2, N1
+UNROLL_D = N1
 
 
 def layer_norm(x):
@@ -152,6 +152,89 @@
     @pl.when(jnp.logical_not(cond))
     def _():
         wait_bytes(ref.at[pl.ds(N0, many)], sem)
+
+
+class Gather:
+    def __init__(self, slab, buf, p1, p2, pz, py, s1, s2, s3):
+        self.slab, self.buf, self.p1, self.p2, self.pz, self.py = slab, buf, p1, p2, pz, py
+        self.s1, self.s2, self.s3 = s1, s2, s3
+        me = my_index()
+        self.me, self.core, chip, self.half = me, lax.rem(me, N2), me // N2, me // N64
+        self.x, self.y, self.z = lax.rem(chip, N4), lax.rem(chip // N4, N4), chip // N16
+        self.mine = self.core == self.half
+        self.level = lax.rem(self.z, N2)
+        self.own = jnp.where(self.core == N0, self.level * N16 + self.y * N4 + self.x, N32 + self.y * N8 + self.x * N2 + self.level)
+
+    def to(self, dz, dy, dx, c):
+        return N2 * (lax.rem(self.z + dz, N4) * N16 + lax.rem(self.y + dy, N4) * N4 + lax.rem(self.x + dx, N4)) + c
+
+    def slots(self, start, n):
+        return self.buf.at[pl.ds(start, n)]
+
+    def first(self):
+        for k in (N1, N3, N2, N0):
+            p = jnp.where(self.core == N0, self.to(N0, N0, k, self.half), self.to(k, N0, N0, self.half))
+
+            @pl.when(p != self.me)
+            def _(p=p):
+                send(self.slab, self.buf.at[self.own], self.s1, self.p1.at[self.core], p)
+
+        @pl.when(self.mine)
+        def _():
+            self.buf[self.own] = self.slab[ALL]
+
+    def second(self):
+        @pl.when(self.mine)
+        def _():
+            ready(self.core == N0, self.buf, N3, N4, self.p1.at[N0])
+            line = self.slots(self.level * N16 + self.y * N4, N4)
+            for k in (N1, N3, N2):
+                send(line, line, self.s2.at[N0], self.p2.at[N0], self.to(N0, k, N0, self.core))
+        ready(jnp.logical_and(self.mine, self.core == N1), self.buf, N1, N2, self.p1.at[N1])
+        pair = self.slots(N32 + self.y * N8 + self.x * N2, N2)
+        for k in (N1, N3, N2):
+            send(pair, pair, self.s2.at[N1], self.p2.at[N1], self.to(N0, N0, k, self.core))
+
+    def third(self):
+        @pl.when(self.mine)
+        def _():
+            wait_bytes(self.slots(N0, 12), self.p2.at[N0])
+            plane = self.slots(self.level * N16, N16)
+            for k in (N1, N3, N2):
+                send(plane, plane, self.s3.at[N0], self.pz.at[self.level], self.to(k, N0, N0, self.core))
+        wait_bytes(self.slots(N0, 6), self.p2.at[N1])
+        row = self.slots(N32 + self.y * N8, N8)
+        for k in (N1, N3, N2):
+            send(row, row, self.s3.at[N1], self.py.at[self.y], self.to(N0, k, N0, self.core))
+
+    def plane_ready(self, level):
+        @pl.when(jnp.logical_not(jnp.logical_and(self.mine, level == self.level)))
+        def _():
+            wait_bytes(self.slots(N0, N16), self.pz.at[level])
+
+    def row_ready(self, y):
+        @pl.when(y != self.y)
+        def _():
+            wait_bytes(self.slots(N0, N8), self.py.at[y])
+
+    def sent(self):
+        ready(self.mine, self.buf, N3, N4, self.s1)
+
+        @pl.when(self.mine)
+        def _():
+            wait_bytes(self.slots(N0, 12), self.s2.at[N0])
+            wait_bytes(self.slots(N0, 48), self.s3.at[N0])
+        wait_bytes(self.slots(N0, 6), self.s2.at[N1])
+        wait_bytes(self.slots(N0, 24), self.s3.at[N1])
+
+
+def slot_device(slot, half):
+    first = slot < N32
+    rest = slot - N32
+    z = jnp.where(first, slot // N16, lax.rem(rest, N2))
+    y = jnp.where(first, lax.rem(slot // N4, N4), rest // N8)
+    x = jnp.where(first, lax.rem(slot, N4), lax.rem(rest // N2, N4))
+    return half * N64 + z * N32 + y * N8 + x * N2 + jnp.where(first, N0, N1)
 
 
 def kernel(scratch_names, m_ref, z_ref, mask_ref, keep_ref, w_row_in, w_row_bias, w_row_out, w_col_in, w_col_out,
@@ -172,19 +255,11 @@
     pl.semaphore_wait(bar, N127)
     send(m_ref, r.xm.at[pl.ds(N2 * core, N2)], r.xsem.at[N0], r.xsem.at[N1], me + N1 - N2 * core)
 
-    def send_slab_a(k):
-        p = N2 * lax.rem(chip + N1 + k, N64) + half
-
-        @pl.when(p != me)
-        def _():
-            send(r.slab_a, r.bias_a.at[slot], r.sa, r.ga.at[slot // N16], p)
-    loop(N64, send_slab_a)
-
-    @pl.when(mine)
-    def _():
-        r.bias_a[slot] = r.slab_a[ALL]
-
+    ga = Gather(r.slab_a, r.bias_a, r.a1, r.a2, r.az3, r.ay3, r.as1, r.as2, r.as3)
+    ga.first()
     r.rep8[ALL] = head_rep(N64, N8)
+    row = iota(N256, N256, N0)
+    r.perm[ALL] = one_hot(iota(N256, N256, N1) == N4 * slot_device(row // N4, N0) + lax.rem(row, N4))
     r.hm8[ALL] = head_mask(N512, N8, N256)
     maskb = mask_ref[ALL].astype(F32).astype(BF16)
     r.rmask[ALL] = dot(one_hot(iota(N4, N256, N1) == N4 * chip + iota(N4, N256, N0)), maskb)
@@ -192,12 +267,15 @@
     lane = iota(N512, N64, N1)
     mask_j = dot(maskb, one_hot(iota(N512, N64, N0) == N32 * lax.rem(lane, N16) + N4 * v + lane // N16)).astype(BF16)
     mask_i = dot(maskb, one_hot(iota(N512, N32, N0) == N32 * u + iota(N512, N32, N1))).astype(BF16)
-    r.recip[ALL] = 1.0 / (1e-3 + dot_c(mask_j, mask_i, N0, N0))
+    recip = 1.0 / (1e-3 + dot_c(mask_j, mask_i, N0, N0))
+    for d in range(N8):
+        r.recip[d] = recip[:, d * N4:(d + N1) * N4]
 
     def project_m(s):
         r.xn_m[ALL] = layer_norm(r.xm[s])
         r.kv_m[s] = dot(r.xn_m[ALL], w_row_in[:, N256:N768]).astype(BF16)
-        xh = r.xn_m[hrows, :]
+        xh = dot(r.perm[ALL], r.xn_m[hrows, :]).astype(BF16)
+        r.x_half[s] = dot(r.perm[ALL], r.xm[s, hrows, :]).astype(BF16)
         r.q_m[s] = dot(xh, w_row_in[:, N0:N256]).astype(BF16)
         r.g_m[s] = dot(xh, w_row_in[:, N768:N1024]).astype(BF16)
 
@@ -205,34 +283,52 @@
         r.xm[N2 * core + s] = m_ref[s]
         project_m(N2 * core + s)
     loop(N2, own_m)
+    ga.second()
     wait_bytes(m_ref, r.xsem.at[N1])
     loop(N2, lambda s: project_m(N2 - N2 * core + s))
-
-    def attend_m(b, s):
+    ga.third()
+
+    def attend_m(b, s, pv):
         rows = pl.ds(pl.multiple_of(b * N64, N64), N64)
         qx = (dot(r.rep8[ALL], r.q_m[s, rows, :]) * r.hm8[ALL]).astype(BF16)
         t = dot_t(qx, r.kv_m[s, :, N0:N256]) * SCALE + r.biasf[ALL]
         t = jnp.where(r.rmask[pl.ds(s, N1), :] > N0, t, LOW)
-        put(r.pv, dot(softmax_rows(t), r.kv_m[s, :, N256:N512]))
-        r.gt_m[s, rows, :] = gate(collapse(r.pv, N64, N8), r.g_m[s, rows, :])
+        put(pv, dot(softmax_rows(t), r.kv_m[s, :, N256:N512]))
+        r.gt_m[s, rows, :] = gate(collapse(pv, N64, N8), r.g_m[s, rows, :])
+
+    def pair_m(b, s2):
+        for e in range(N2):
+            attend_m(b, N2 * s2 + e, r.pv.at[e])
 
     def finish_m(b, s):
         rows = pl.ds(pl.multiple_of(b * N64, N64), N64)
-        put(r.y_m, r.xm[s, pl.ds(pl.multiple_of(core * N256 + b * N64, N64), N64), :].astype(F32) + dot(r.gt_m[s, rows, :], w_row_out[ALL]))
+        put(r.y_m, r.x_half[s, rows, :].astype(F32) + dot(r.gt_m[s, rows, :], w_row_out[ALL]))
         for jl in range(N4):
             spread(r.f_b, s * N4 + jl, N16, N16, take(r.y_m, jl, N16, N4))
 
     def block_m(step):
-        b = lax.rem(jnp.where(chip // N32 == core, (chip - N32 * core) // N8, N0) + N3 - step, N4)
-        ready(jnp.logical_and(mine, b == slot // N16), r.bias_a, N15, N16, r.ga.at[b])
+        late = jnp.where(mine, N0, N2)
+        planes = jnp.logical_or(step == late, step == N3)
+        level = jnp.where(step == late, ga.level, N1 - ga.level)
+        two = jnp.where(step == N1 - late // N2, ga.y // N2, N1 - ga.y // N2)
+        b = jnp.where(planes, level, N2 + two)
+
+        @pl.when(planes)
+        def _():
+            ga.plane_ready(level)
+
+        @pl.when(jnp.logical_not(planes))
+        def _():
+            for e in range(N2):
+                ga.row_ready(N2 * two + e)
         r.biasf[ALL] = r.bias_a[pl.ds(b * N16, N16)].reshape(N512, N512).astype(F32) * LOG2E
-        loop(N4, lambda s: attend_m(b, s), UNROLL_A)
+        loop(N2, lambda s2: pair_m(b, s2))
         loop(N4, lambda s: finish_m(b, s))
         r.send_m[pl.ds(b * N16, N16)] = join(r.f_b).astype(BF16).reshape(N16, N16, N256)
 
         def send_cols_m(k0):
-            k = b * N16 + lax.rem(slot + N1 + k0, N16)
-            q = N64 * core + k
+            k = b * N16 + lax.rem(ga.own + N1 + k0, N16)
+            q = slot_device(k, core)
 
             @pl.when(q != me)
             def _():
@@ -242,7 +338,7 @@
 
     @pl.when(mine)
     def _():
-        r.recv_m[chip] = r.send_m[slot]
+        r.recv_m[chip] = r.send_m[ga.own]
 
     r.bd[ALL] = jnp.zeros_like(r.bd)
     r.wf[ALL] = w_opm_out[ALL].astype(F32)
@@ -255,8 +351,6 @@
     loop(N16, build)
     r.rep4[ALL] = head_rep(N128, N4)
     r.hm4[ALL] = head_mask(N512, N4, N128)
-    r.rept[ALL] = one_hot(iota(N128, N512, N1) // N4 == iota(N128, N512, N0))
-    r.hmt[ALL] = (lax.rem(iota(N128, N512, N1), N4) == iota(N128, N512, N0) // N32).astype(F32)
     for e in range(N2):
         r.wet[e] = jnp.transpose(w_e_in[:, N256 + e * N128:N384 + e * N128].astype(F32)).astype(BF16)
     keep = jnp.where(iota(N8, N512, N0) == N0, keep_ref[ALL].astype(F32), 0.0).astype(BF16)
@@ -284,14 +378,13 @@
         x = take(r.xs_m, jl, N256, N4)
         r.qkvg[ALL] = dot(layer_norm(x), w_col_in[ALL]).astype(BF16)
 
-        def col_block(b, jl=jl):
-            rows = pl.ds(pl.multiple_of(b * N64, N64), N64)
+        for b in range(N4):
+            rows, pv = slice(b * N64, (b + N1) * N64), r.pv.at[b]
             qx = (dot(r.rep8[ALL], r.qkvg[rows, N0:N256]) * r.hm8[ALL]).astype(BF16)
             t = dot_t(qx, r.qkvg[:, N256:N512]) * SCALE
             t = jnp.where(r.cmask[jl:jl + N1, :] > N0, t, LOW)
-            put(r.pv, dot(softmax_rows(t), r.qkvg[:, N512:N768]))
-            r.gt_m[N0, rows, :] = gate(collapse(r.pv, N64, N8), r.qkvg[rows, N768:N1024])
-        loop(N4, col_block, UNROLL_B)
+            put(pv, dot(softmax_rows(t), r.qkvg[:, N512:N768]))
+            r.gt_m[N0, rows, :] = gate(collapse(pv, N64, N8), r.qkvg[rows, N768:N1024])
         y = (x + dot(r.gt_m[N0], w_col_out[ALL])).astype(BF16)
         spread(r.yf_m, jl, N256, N4, y.astype(F32))
         ab = dot_t(layer_norm(y), w_opm_in[ALL]).astype(BF16)
@@ -310,7 +403,6 @@
         r.lall[v, jl] = r.left[jl]
 
     r.mcols[ALL] = join(r.yf_m).astype(BF16).reshape(N128, N8, N256)
-    r.acc[ALL] = jnp.zeros_like(r.acc)
     wait_bytes(r.rall.at[:, pl.ds(N0, N15)], r.csem.at[N1])
     wait_bytes(r.lall.at[pl.ds(N0, N7)], r.lsem.at[N1])
 
@@ -320,25 +412,36 @@
         r.rc[c] = take(r.rf, c, N64, N32).astype(BF16)
     loop(N32, reorder, N4)
 
-    def outer(d):
-        r.o[d] = dot_t(r.rc[ALL].reshape(N2048, N256), r.lall[d].reshape(N128, N256)).astype(BF16).reshape(N32, N64, N128)
-    loop(N8, outer)
-
-    def mix(c2):
-        parts = [r.o[:, N2 * c2 + e].reshape(N512, N128) for e in range(N2)]
-        r.acc[ALL] += dot(jnp.concatenate(parts, axis=N1), r.bd[c2])
-    loop(N16, mix)
     wait_bytes(r.zin.at[pl.ds(N0, N7)], r.zsem.at[N1])
-    for d in range(N8):
-        for il in range(N4):
-            cols = slice(il * N128, (il + N1) * N128)
-            upd = r.acc[d * N64:(d + N1) * N64, cols] * r.recip[:, d * N4 + il:d * N4 + il + N1]
-            r.zs[d, :, cols] = (r.zin[d, :, cols].astype(F32) + upd).astype(BF16)
-
-    def send_z(k):
-        d = lax.rem(v + N1 + k, N8)
-        send(r.zs.at[d], r.zback.at[v], r.bsem.at[N0], r.bsem.at[N1], u * N8 + d)
-    loop(N7, send_z)
+
+    def group(g):
+        def outer(t):
+            d = lax.rem(v + N1 + N4 * g + t, N8)
+            r.o[t] = dot_t(r.rc[ALL].reshape(N2048, N256), r.lall[d].reshape(N128, N256)).astype(BF16).reshape(N32, N64, N128)
+        loop(N4, outer)
+
+        def mix(c4):
+            total = None
+            for e in range(N4):
+                c = c4 * N8 + N2 * e
+                part = dot(jnp.concatenate([r.o[:, c].reshape(N256, N128), r.o[:, c + N1].reshape(N256, N128)], axis=N1), r.bd[c4 * N4 + e])
+                total = part if total is None else total + part
+            r.acc[ALL] = jnp.where(c4 == N0, 0.0, r.acc[ALL]) + total
+        loop(N4, mix)
+
+        def update(t):
+            d = lax.rem(v + N1 + N4 * g + t, N8)
+            rows = pl.ds(pl.multiple_of(t * N64, N64), N64)
+            for il in range(N4):
+                cols = slice(il * N128, (il + N1) * N128)
+                upd = r.acc[rows, cols] * r.recip[d, :, il:il + N1]
+                r.zs[d, :, cols] = (r.zin[d, :, cols].astype(F32) + upd).astype(BF16)
+
+            @pl.when(d != v)
+            def _():
+                send(r.zs.at[d], r.zback.at[v], r.bsem.at[N0], r.bsem.at[N1], u * N8 + d)
+        loop(N4, update)
+    loop(N2, group)
     r.zback[v] = r.zs[v]
     wait_bytes(r.zback.at[pl.ds(N0, N7)], r.bsem.at[N1])
 
@@ -365,12 +468,6 @@
     @pl.when(mine)
     def _():
         r.bias_s[slot] = r.slab_s[ALL]
-
-    def send_m_out(k):
-        p = lax.rem(me + N1 + k, N128)
-        send(r.mcols.at[p], r.mback.at[me], r.msem.at[N0], r.msem.at[N1], p)
-    loop(N127, send_m_out)
-    r.mback[me] = r.mcols[me]
 
     def project_z(i):
         r.xn_z[ALL] = layer_norm(r.xz[i])
@@ -388,26 +485,36 @@
     wait_bytes(r.zb, r.ysem.at[N1])
     loop(N4, lambda i: project_z(N4 - N4 * core + i))
 
-    def attend_z(b, i):
+    def send_m_out(k):
+        p = lax.rem(me + N1 + k, N128)
+        send(r.mcols.at[p], r.mback.at[me], r.msem.at[N0], r.msem.at[N1], p)
+    loop(N127, send_m_out)
+    r.mback[me] = r.mcols[me]
+
+    def attend_z(b, i, pv):
         rows = pl.ds(pl.multiple_of(b * N128, N128), N128)
         qx = (dot(r.rep4[ALL], r.q_z[i, rows, :]) * r.hm4[ALL]).astype(BF16)
         t = dot_t(qx, r.kv_z[i, :, N0:N128]) * SCALE + r.biasf[ALL]
-        r.pv[N0] = dot(softmax_rows(t), r.kv_z[i, :, N128:N256])
-        r.gt_z[i, rows, :] = gate(collapse(r.pv.at[N0:N1], N128, N4), r.g_z[i, rows, :])
+        put(pv, dot(softmax_rows(t), r.kv_z[i, :, N128:N256]))
+        r.gt_z[i, rows, :] = gate(collapse(pv, N128, N4), r.g_z[i, rows, :])
+
+    def pair_z(b, i2):
+        for e in range(N2):
+            attend_z(b, N2 * i2 + e, r.pv.at[e, N0:N1])
 
     def block_z(step):
         b = lax.rem(jnp.where(chip // N32 == core, (chip - N32 * core) // N16, N0) + N1 + step, N2)
         ready(jnp.logical_and(mine, b == slot // N32), r.bias_s, 31, N32, r.gs.at[b])
         got = r.bias_s[pl.ds(b * N32, N32)].reshape(N512, N512).astype(F32)
         r.biasf[ALL] = jnp.where(r.keepr[ALL] > N0, got * LOG2E, LOW)
-        loop(N8, lambda i: attend_z(b, i), UNROLL_C)
+        loop(N4, lambda i2: pair_z(b, i2))
     loop(N2, block_z)
 
     for i in range(N8):
         y = (r.xz[i, hrows, :].astype(F32) + dot(r.gt_z[i], w_s_out[ALL])).astype(BF16)
         r.f_z[:, i] = y.astype(F32).reshape(N32, N8, N128)
-        r.e_f[i * N4:(i + N1) * N4, N0:N256] = dot_t(w_e_bias[ALL], layer_norm(y))
-    r.slab_e[ALL] = r.e_f[:, N0:N256].astype(BF16)
+        spread(r.e_b, i, N4, N8, dot_t(w_e_bias[ALL], layer_norm(y)))
+    r.slab_e[ALL] = join(r.e_b).astype(BF16)
     r.send_zc[ALL] = r.f_z[ALL].astype(BF16).reshape(N32, N64, N128)
 
     def send_cols_z(k0):
@@ -452,25 +559,26 @@
     wait_bytes(r.bias_e.at[pl.ds(N0, N63)], r.esem.at[N1])
 
     def widen(b):
-        rows = pl.ds(pl.multiple_of(b * N512, N512), N512)
-        kept = dot(r.rep4[ALL], r.keepc[pl.ds(pl.multiple_of(b * N128, N128), N128), :].astype(BF16))
-        got = r.bias_e[pl.ds(b * N16, N16)].reshape(N512, N256).astype(F32)
-        for t in range(N2):
-            r.biasf_e[rows, t * N128:(t + N1) * N128] = jnp.where(kept > N0, got[:, t * N128:(t + N1) * N128] * LOG2E, LOW)
+        rows = pl.ds(pl.multiple_of(b * N128, N128), N128)
+        kept = r.keepc[rows, :].reshape(N16, N8, N128)
+        got = r.bias_e[pl.ds(b * N16, N16)].astype(F32).reshape(N16, N4, N8, N256) * LOG2E
+        for h in range(N4):
+            for t in range(N2):
+                lanes = slice(t * N128, (t + N1) * N128)
+                r.biasf_e[h, rows, lanes] = jnp.where(kept > N0, got[:, h, :, lanes], LOW).reshape(N128, N128)
     loop(N4, widen)
 
     def column(j):
-        for b in range(N4):
-            r.kx[b * N512:(b + N1) * N512, :] = (dot(r.rep4[ALL], r.k_e[j, b * N128:(b + N1) * N128, :]) * r.hm4[ALL]).astype(BF16)
-            r.vx[:, b * N512:(b + N1) * N512] = (dot(r.v_e[j, :, b * N128:(b + N1) * N128], r.rept[ALL]) * r.hmt[ALL]).astype(BF16)
-        t = (dot_t(r.kx[ALL], r.q_z[j]) * SCALE + r.biasf_e[ALL]).reshape(N256, N8, N256)
-        top = jnp.max(t, axis=N0)
-        top = jnp.maximum(top, pltpu.roll(top, N4, N0))
-        e = jnp.exp2(t - top[None])
-        total = jnp.sum(e, axis=N0)
-        total = total + pltpu.roll(total, N4, N0)
-        p = (e * (1.0 / total)[None]).astype(BF16).reshape(N2048, N256)
-        gated = gate(dot(r.vx[ALL], p), r.g_e[j])
+        lane = iota(N256, N128, N1) // N32
+        row = iota(N128, N512, N0) // N32
+        probs, values = [], []
+        for h in range(N4):
+            qh = jnp.where(lane == h, r.q_z[j].astype(F32), 0.0).astype(BF16)
+            t = dot_t(r.k_e[j], qh) * SCALE + r.biasf_e[h]
+            e = jnp.exp2(t - jnp.max(t, axis=N0, keepdims=True))
+            probs.append((e * (1.0 / jnp.sum(e, axis=N0, keepdims=True))).astype(BF16))
+            values.append(jnp.where(row == h, r.v_e[j].astype(F32), 0.0).astype(BF16))
+        gated = gate(dot(jnp.concatenate(values, axis=N1), jnp.concatenate(probs, axis=N0)), r.g_e[j])
         y = dot_c(gated, w_e_out[ALL], N0, N0)
         r.y_z[pl.ds(j, N256, stride=N8), :] = r.xs_z[pl.ds(core * N2048 + j, N256, stride=N8), :] + y
     loop(N8, column, UNROLL_D)
@@ -488,8 +596,9 @@
     @pl.when(mine)
     def _():
         r.recv_o[chip] = r.send_o[slot]
-    for ref, sem in ((r.bias_a, r.sa), (r.recv_m, r.am.at[N0]), (r.bias_s, r.ss)):
-        ready(mine, ref, N63, N64, sem)
+    ga.sent()
+    ready(mine, r.recv_m, N63, N64, r.am.at[N0])
+    ready(mine, r.bias_s, N63, N64, r.ss)
     ready(mine, r.recv_zc, 31, N32, r.az.at[N0])
     wait_bytes(taken, r.fsem.at[N0])
     wait_bytes(m_ref, r.xsem.at[N0])
@@ -509,19 +618,19 @@
 
 BUFFERS = dict(
     slab_a=(N32, N512), bias_a=(N64, N32, N512), xm=(N4, N512, N256), xn_m=(N512, N256), kv_m=(N4, N512, N512), q_m=(N4, N256, N256),
-    g_m=(N4, N256, N256), gt_m=(N4, N256, N256), rep8=(N512, N64), zsplit=(N8, N64, N512), zin=(N8, N64, N512), send_m=(N64, N16, N256),
+    g_m=(N4, N256, N256), gt_m=(N4, N256, N256), rep8=(N512, N64), perm=(N256, N256), x_half=(N4, N256, N256), zsplit=(N8, N64, N512), zin=(N8, N64, N512), send_m=(N64, N16, N256),
     recv_m=(N64, N16, N256), qkvg=(N256, N1024), left=(N4, N32, N256), right=(N4, N32, N256), lall=(N8, N4, N32, N256), rall=(N4, N16, N32, N256),
-    mcols=(N128, N8, N256), o=(N8, N32, N64, N128), rc=(N32, N64, N256), mback=(N128, N8, N256), bd=(N16, N256, N512), zs=(N8, N64, N512), zback=(N8, N64, N512), zb=(N4, N512, N128),
+    mcols=(N128, N8, N256), o=(N4, N32, N64, N128), rc=(N32, N64, N256), mback=(N128, N8, N256), bd=(N16, N256, N512), zs=(N8, N64, N512), zback=(N8, N64, N512), zb=(N4, N512, N128),
     xz=(N8, N512, N128), slab_s=(N16, N512), bias_s=(N64, N16, N512), xn_z=(N512, N128), kv_z=(N8, N512, N256), q_z=(N8, N256, N128),
-    g_z=(N8, N256, N128), gt_z=(N8, N256, N128), rep4=(N512, N128), rept=(N128, N512), wet=(N2, N128, N128), slab_e=(N32, N256),
-    bias_e=(N64, N32, N256), send_zc=(N32, N64, N128), recv_zc=(N64, N64, N128), k_e=(N8, N512, N128), v_e=(N8, N128, N512), g_e=(N8, N128, N256), kx=(N2048, N128), vx=(N128, N2048),
+    g_z=(N8, N256, N128), gt_z=(N8, N256, N128), rep4=(N512, N128), wet=(N2, N128, N128), slab_e=(N32, N256),
+    bias_e=(N64, N32, N256), send_zc=(N32, N64, N128), recv_zc=(N64, N64, N128), k_e=(N8, N512, N128), v_e=(N8, N128, N512), g_e=(N8, N128, N256),
     send_o=(N64, N32, N128), recv_o=(N64, N32, N128))
 FLOATS = dict(
-    slab_f=(N32, N512), rmask=(N4, N512), cmask=(N4, N256), recip=(N64, N32), hm8=(N512, N256), hm4=(N512, N128),
-    hmt=(N128, N512), keepc=(N512, N128), keepr=(N1, N512), zf=(N4, N512, N128), pv=(N2, N512, N128), y_m=(N2, N64, N128), f_b=(N2, N256, N128),
-    f_m=(N2, N1024, N128), xs_m=(N2, N1024, N128), yf_m=(N2, N1024, N128), wf=(N1024, N128), rf=(N2, N2048, N128), acc=(N512, N512),
-    e_f=(N32, N512), biasf=(N512, N512), f_z=(N32, N8, N8, N128), biasf_e=(N2048, N256), xs_z=(N4096, N128), y_z=(N2048, N128))
-SEMS = dict(ga=N4, gs=N2, xsem=N2, ysem=N2, zsem=N2, am=N2, csem=N2, lsem=N2, bsem=N2, msem=N2, az=N2, fsem=N2, esem=N2, osem=N2, sa=None, ss=None)
+    slab_f=(N32, N512), rmask=(N4, N512), cmask=(N4, N256), recip=(N8, N64, N4), hm8=(N512, N256), hm4=(N512, N128),
+    keepc=(N512, N128), keepr=(N1, N512), zf=(N4, N512, N128), pv=(N4, N2, N512, N128), y_m=(N2, N64, N128), f_b=(N2, N256, N128),
+    f_m=(N2, N1024, N128), xs_m=(N2, N1024, N128), yf_m=(N2, N1024, N128), wf=(N1024, N128), rf=(N2, N2048, N128), acc=(N256, N512),
+    e_f=(N32, N512), biasf=(N512, N512), f_z=(N32, N8, N8, N128), biasf_e=(N4, N512, N256), e_b=(N2, N32, N128), xs_z=(N4096, N128), y_z=(N2048, N128))
+SEMS = dict(a1=N2, a2=N2, az3=N2, ay3=N4, as1=None, as2=N2, as3=N2, gs=N2, ss=None, xsem=N2, ysem=N2, zsem=N2, am=N2, csem=N2, lsem=N2, bsem=N2, msem=N2, az=N2, fsem=N2, esem=N2, osem=N2)
 
 
 def solution(mesh):

time: 192 us -> 166 us (0.86)
  Pallas kernels: 189 us -> 162 us
    pallas_call x1, Pallas kernels: 189 us -> 162 us  [per_device(): pl.pallas_call(functools.partial(kernel, tuple(specs)), out_shape=(jax.Sh...]
where the time goes in v4:
time: 166 us
  Pallas kernels  162 us (98%)
  local copies, waits for them, and re-layouts  2.72 us (2%)
    pallas_call x1, Pallas kernels, per_device(): pl.pallas_call(functools.partial(kernel, tuple(specs)), out_shape=(jax.Sh...  162 us

profile of v4, /device:TPU:1, one launch (start us, length us, event | category | flops | bytes accessed | tf_op | source)
XLA Modules:
  0.0 165.8 jit_solution(10198154256482849662)
XLA Ops:
  0.6 162.4 %shard_map.176 = (bf16[2,512,256]{2,1,0:T(8,128)(2,1)}, bf16[4,512,128]{2,1,0:T(8,128)(2,1)}) custom-call(bf16[2,512,256]{2,1,0:T(8,128)(2,1)} %m_ref.1, bf16[4,512,128]{2,1,0:T(8,128)(2,1)} %z_ref.1, s32[256,512]{1,0:T(8,128)} %mask_ref.1, s32[1,512]{1,0:T(1,128)} %bitcast.6, bf16[256,1024]{1,0:T(8,128)(2,1)} %w_row_in.1, bf16[8,128]{1,0:T(8,128)(2,1)} %bitcast.7, ...), custom_call_target="tpu_custom_call" | custom-call | tf_op jit(solution)/shard_map/pallas_call | solution.py:649
  163.1 0.0 copy-start
  163.1 1.9 %copy.21 = bf16[2,512,256]{2,1,0:T(8,128)(2,1)} copy(bf16[2,512,256]{2,1,0:T(8,128)(2,1)} %get-tuple-element.4) | data formatting | bytes 1048576
  165.0 0.0 copy-done
  165.0 0.8 copy.22
Async XLA Ops:
  163.1 1.9 %copy-start = (bf16[4,512,128]{2,1,0:T(8,128)(2,1)S(1)}, bf16[4,512,128]{2,1,0:T(8,128)(2,1)}, u32[]{:S(2)}) copy-start(bf16[4,512,128]{2,1,0:T(8,128)(2,1)} %get-tuple-element.5) | copy-start | bytes 1572868

commit v5 on v4

--- a/solution.py
+++ b/solution.py
@@ -34,7 +34,6 @@
 F32 = jnp.float32
 BF16 = jnp.bfloat16
 VMEM_LIMIT = 67043328
-UNROLL_D = N1
 
 
 def layer_norm(x):
@@ -121,6 +120,22 @@
             out = jnp.where(lane == h, r_ref[t, pl.ds(N4 * t + h, queries, stride=heads), :], out)
         parts.append(out)
     return jnp.concatenate(parts, axis=N1) if len(parts) > N1 else parts[N0]
+
+
+def softmax_cols(t):
+    e = jnp.exp2(t - jnp.max(t, axis=N0, keepdims=True))
+    return (e * (1.0 / jnp.sum(e, axis=N0, keepdims=True))).astype(BF16)
+
+
+def heads_attend(queries, keys, values, logits):
+    lane, row = iota(*queries.shape, N1) // N32, iota(*values.shape, N0) // N32
+    wide_q, wide_v = queries.astype(F32), values.astype(F32)
+    probs, parts = [], []
+    for h in range(N4):
+        scores = dot_t(keys, jnp.where(lane == h, wide_q, 0.0).astype(BF16)) * SCALE
+        probs.append(softmax_cols(logits(h, scores)))
+        parts.append(jnp.where(row == h, wide_v, 0.0).astype(BF16))
+    return dot(jnp.concatenate(parts, axis=N1), jnp.concatenate(probs, axis=N0))
 
 
 def gate(o, g):
@@ -252,17 +267,21 @@
     for il in range(N4):
         r.slab_f[il * N8:(il + N1) * N8, :] = dot_t(w_row_bias[ALL], layer_norm(z_ref[il]))
     r.slab_a[ALL] = r.slab_f[ALL].astype(BF16)
+    for e in range(N2):
+        lanes = slice(N512 + e * N256, N768 + e * N256)
+        r.wrt[e] = jnp.transpose(w_row_in[:, lanes].astype(F32)).astype(BF16)
     pl.semaphore_wait(bar, N127)
     send(m_ref, r.xm.at[pl.ds(N2 * core, N2)], r.xsem.at[N0], r.xsem.at[N1], me + N1 - N2 * core)
 
     ga = Gather(r.slab_a, r.bias_a, r.a1, r.a2, r.az3, r.ay3, r.as1, r.as2, r.as3)
     ga.first()
-    r.rep8[ALL] = head_rep(N64, N8)
     row = iota(N256, N256, N0)
     r.perm[ALL] = one_hot(iota(N256, N256, N1) == N4 * slot_device(row // N4, N0) + lax.rem(row, N4))
-    r.hm8[ALL] = head_mask(N512, N8, N256)
     maskb = mask_ref[ALL].astype(F32).astype(BF16)
-    r.rmask[ALL] = dot(one_hot(iota(N4, N256, N1) == N4 * chip + iota(N4, N256, N0)), maskb)
+    wide = dot_c(maskb, one_hot(iota(N256, N512, N0) == N4 * chip + iota(N256, N512, N1) // N128), N0, N0)
+    for e in range(N4):
+        r.rmask[e] = wide[:, e * N128:(e + N1) * N128]
+        r.cmaskc[e] = dot(maskb, one_hot(iota(N512, N128, N0) == N4 * me + e))
     r.cmask[ALL] = dot_c(one_hot(iota(N4, N512, N1) == N4 * me + iota(N4, N512, N0)), maskb, N1, N1)
     lane = iota(N512, N64, N1)
     mask_j = dot(maskb, one_hot(iota(N512, N64, N0) == N32 * lax.rem(lane, N16) + N4 * v + lane // N16)).astype(BF16)
@@ -273,11 +292,14 @@
 
     def project_m(s):
         r.xn_m[ALL] = layer_norm(r.xm[s])
-        r.kv_m[s] = dot(r.xn_m[ALL], w_row_in[:, N256:N768]).astype(BF16)
+        r.k_m[s] = dot(r.xn_m[ALL], w_row_in[:, N256:N512]).astype(BF16)
+        r.v_m[s] = dot_t(r.wrt[N0], r.xn_m[ALL]).astype(BF16)
         xh = dot(r.perm[ALL], r.xn_m[hrows, :]).astype(BF16)
         r.x_half[s] = dot(r.perm[ALL], r.xm[s, hrows, :]).astype(BF16)
         r.q_m[s] = dot(xh, w_row_in[:, N0:N256]).astype(BF16)
-        r.g_m[s] = dot(xh, w_row_in[:, N768:N1024]).astype(BF16)
+        g = dot_t(r.wrt[N1], xh).astype(BF16)
+        r.g_m[N0, s] = g[:, N0:N128]
+        r.g_m[N1, s] = g[:, N128:N256]
 
     def own_m(s):
         r.xm[N2 * core + s] = m_ref[s]
@@ -288,53 +310,45 @@
     loop(N2, lambda s: project_m(N2 - N2 * core + s))
     ga.third()
 
-    def attend_m(b, s, pv):
-        rows = pl.ds(pl.multiple_of(b * N64, N64), N64)
-        qx = (dot(r.rep8[ALL], r.q_m[s, rows, :]) * r.hm8[ALL]).astype(BF16)
-        t = dot_t(qx, r.kv_m[s, :, N0:N256]) * SCALE + r.biasf[ALL]
-        t = jnp.where(r.rmask[pl.ds(s, N1), :] > N0, t, LOW)
-        put(pv, dot(softmax_rows(t), r.kv_m[s, :, N256:N512]))
-        r.gt_m[s, rows, :] = gate(collapse(pv, N64, N8), r.g_m[s, rows, :])
-
-    def pair_m(b, s2):
-        for e in range(N2):
-            attend_m(b, N2 * s2 + e, r.pv.at[e])
-
-    def finish_m(b, s):
-        rows = pl.ds(pl.multiple_of(b * N64, N64), N64)
-        put(r.y_m, r.x_half[s, rows, :].astype(F32) + dot(r.gt_m[s, rows, :], w_row_out[ALL]))
-        for jl in range(N4):
-            spread(r.f_b, s * N4 + jl, N16, N16, take(r.y_m, jl, N16, N4))
-
-    def block_m(step):
-        late = jnp.where(mine, N0, N2)
-        planes = jnp.logical_or(step == late, step == N3)
-        level = jnp.where(step == late, ga.level, N1 - ga.level)
-        two = jnp.where(step == N1 - late // N2, ga.y // N2, N1 - ga.y // N2)
-        b = jnp.where(planes, level, N2 + two)
-
-        @pl.when(planes)
-        def _():
-            ga.plane_ready(level)
-
-        @pl.when(jnp.logical_not(planes))
-        def _():
-            for e in range(N2):
-                ga.row_ready(N2 * two + e)
-        r.biasf[ALL] = r.bias_a[pl.ds(b * N16, N16)].reshape(N512, N512).astype(F32) * LOG2E
-        loop(N2, lambda s2: pair_m(b, s2))
-        loop(N4, lambda s: finish_m(b, s))
-        r.send_m[pl.ds(b * N16, N16)] = join(r.f_b).astype(BF16).reshape(N16, N16, N256)
+    def block_m(b):
+        if b == N1:
+            for y in range(N4):
+                ga.row_ready(y)
+        else:
+            for level in range(N2):
+                ga.plane_ready(level)
+        put(r.wide_a, r.bias_a[pl.ds(b * N32, N32)].astype(F32).reshape(N1024, N512))
+
+        def turn(h):
+            for t in range(N4):
+                r.bias_t[h, t * N128:(t + N1) * N128, :] = jnp.transpose(r.wide_a[t, pl.ds(h, N128, stride=N8), :]) * LOG2E
+        loop(N8, turn)
+
+        def attend_m(s):
+            kept = r.rmask[s] > N0
+            rows = slice(b * N128, (b + N1) * N128)
+            parts = []
+            for t in range(N2):
+                lanes = slice(t * N128, (t + N1) * N128)
+                parts.append(heads_attend(r.q_m[s, rows, lanes], r.k_m[s, :, lanes], r.v_m[s, lanes, :],
+                                          lambda h, x, t=t: jnp.where(kept, x + r.bias_t[N4 * t + h], LOW)))
+            gated = gate(jnp.concatenate(parts, axis=N0), r.g_m[b, s])
+            put(r.y_m, r.x_half[s, rows, :].astype(F32) + dot_c(gated, w_row_out[ALL], N0, N0))
+            for jl in range(N4):
+                spread(r.f_b, s * N4 + jl, N32, N16, take(r.y_m, jl, N32, N4))
+        loop(N4, attend_m)
+        r.send_m[b * N32:(b + N1) * N32] = join(r.f_b).astype(BF16).reshape(N32, N16, N256)
 
         def send_cols_m(k0):
-            k = b * N16 + lax.rem(ga.own + N1 + k0, N16)
+            k = b * N32 + lax.rem(ga.own + N1 + k0, N32)
             q = slot_device(k, core)
 
             @pl.when(q != me)
             def _():
                 send(r.send_m.at[k], r.recv_m.at[chip], r.am.at[N0], r.am.at[N1], q)
-        loop(N16, send_cols_m)
-    loop(N4, block_m)
+        loop(N32, send_cols_m)
+    block_m(N1)
+    block_m(N0)
 
     @pl.when(mine)
     def _():
@@ -365,6 +379,9 @@
                 r.zsplit[d, jl * N16:(jl + N1) * N16, il * N128:(il + N1) * N128] = r.zf[il, pl.ds(d * N4 + jl, N16, stride=N32), :].astype(BF16)
     loop(N8, split_z)
 
+    for e in range(N2):
+        lanes = slice(N512 + e * N256, N768 + e * N256)
+        r.wct[e] = jnp.transpose(w_col_in[:, lanes].astype(F32)).astype(BF16)
     ready(mine, r.recv_m, N63, N64, r.am.at[N1])
     def send_z_in(k):
         d = lax.rem(v + N1 + k, N8)
@@ -376,16 +393,17 @@
 
     for jl in range(N4):
         x = take(r.xs_m, jl, N256, N4)
-        r.qkvg[ALL] = dot(layer_norm(x), w_col_in[ALL]).astype(BF16)
-
-        for b in range(N4):
-            rows, pv = slice(b * N64, (b + N1) * N64), r.pv.at[b]
-            qx = (dot(r.rep8[ALL], r.qkvg[rows, N0:N256]) * r.hm8[ALL]).astype(BF16)
-            t = dot_t(qx, r.qkvg[:, N256:N512]) * SCALE
-            t = jnp.where(r.cmask[jl:jl + N1, :] > N0, t, LOW)
-            put(pv, dot(softmax_rows(t), r.qkvg[:, N512:N768]))
-            r.gt_m[N0, rows, :] = gate(collapse(pv, N64, N8), r.qkvg[rows, N768:N1024])
-        y = (x + dot(r.gt_m[N0], w_col_out[ALL])).astype(BF16)
+        xn = layer_norm(x)
+        qk = dot(xn, w_col_in[:, N0:N512]).astype(BF16)
+        vt = dot_t(r.wct[N0], xn).astype(BF16)
+        gt = dot_t(r.wct[N1], xn).astype(BF16)
+        kept = jnp.concatenate([r.cmaskc[jl], r.cmaskc[jl]], axis=N1) > N0
+        parts = []
+        for t in range(N2):
+            lanes = slice(t * N128, (t + N1) * N128)
+            parts.append(heads_attend(qk[:, lanes], qk[:, N256 + t * N128:N384 + t * N128], vt[lanes, :],
+                                      lambda h, y, kept=kept: jnp.where(kept, y, LOW)))
+        y = (x + dot_c(gate(jnp.concatenate(parts, axis=N0), gt), w_col_out[ALL], N0, N0)).astype(BF16)
         spread(r.yf_m, jl, N256, N4, y.astype(F32))
         ab = dot_t(layer_norm(y), w_opm_in[ALL]).astype(BF16)
         for side, ref in ((N0, r.left), (N1, r.right)):
@@ -485,11 +503,6 @@
     wait_bytes(r.zb, r.ysem.at[N1])
     loop(N4, lambda i: project_z(N4 - N4 * core + i))
 
-    def send_m_out(k):
-        p = lax.rem(me + N1 + k, N128)
-        send(r.mcols.at[p], r.mback.at[me], r.msem.at[N0], r.msem.at[N1], p)
-    loop(N127, send_m_out)
-    r.mback[me] = r.mcols[me]
 
     def attend_z(b, i, pv):
         rows = pl.ds(pl.multiple_of(b * N128, N128), N128)
@@ -534,13 +547,6 @@
         send(r.slab_e, r.bias_e.at[chip], r.esem.at[N0], r.esem.at[N1], N2 * lax.rem(chip + N1 + k0, N64) + core)
     loop(N63, send_slab_e)
     r.bias_e[chip] = r.slab_e[ALL]
-
-    wait_bytes(r.mback.at[pl.ds(N0, N127)], r.msem.at[N1])
-    put(r.yf_m, r.mback[ALL].astype(F32).reshape(N1024, N256))
-    for sl in range(N2):
-        for jl in range(N4):
-            spread(r.f_m, sl * N512 + jl, N128, N4, take(r.yf_m, sl * N4 + jl, N128, N8))
-    m_out[ALL] = join(r.f_m).astype(BF16).reshape(N2, N512, N256)
 
     ready(mine, r.recv_zc, 31, N32, r.az.at[N1])
     taken = r.recv_zc.at[pl.ds(N32 * core, N32)]
@@ -568,34 +574,33 @@
                 r.biasf_e[h, rows, lanes] = jnp.where(kept > N0, got[:, h, :, lanes], LOW).reshape(N128, N128)
     loop(N4, widen)
 
-    def column(j):
-        lane = iota(N256, N128, N1) // N32
-        row = iota(N128, N512, N0) // N32
-        probs, values = [], []
-        for h in range(N4):
-            qh = jnp.where(lane == h, r.q_z[j].astype(F32), 0.0).astype(BF16)
-            t = dot_t(r.k_e[j], qh) * SCALE + r.biasf_e[h]
-            e = jnp.exp2(t - jnp.max(t, axis=N0, keepdims=True))
-            probs.append((e * (1.0 / jnp.sum(e, axis=N0, keepdims=True))).astype(BF16))
-            values.append(jnp.where(row == h, r.v_e[j].astype(F32), 0.0).astype(BF16))
-        gated = gate(dot(jnp.concatenate(values, axis=N1), jnp.concatenate(probs, axis=N0)), r.g_e[j])
+    def send_m_out(k):
+        p = lax.rem(me + N1 + k, N128)
+        send(r.mcols.at[p], r.mback.at[me], r.msem.at[N0], r.msem.at[N1], p)
+    loop(N127, send_m_out)
+    r.mback[me] = r.mcols[me]
+    def column(part, j4):
+        j = N4 * part + j4
+        gated = gate(heads_attend(r.q_z[j], r.k_e[j], r.v_e[j], lambda h, x: x + r.biasf_e[h]), r.g_e[j])
         y = dot_c(gated, w_e_out[ALL], N0, N0)
-        r.y_z[pl.ds(j, N256, stride=N8), :] = r.xs_z[pl.ds(core * N2048 + j, N256, stride=N8), :] + y
-    loop(N8, column, UNROLL_D)
-    r.send_o[ALL] = r.y_z[ALL].astype(BF16).reshape(N64, N32, N128)
-
-    def send_back(k0):
-        k = lax.rem(slot + N1 + k0, N64)
-        q = N64 * core + k
-
-        @pl.when(q != me)
-        def _():
-            send(r.send_o.at[k], r.recv_o.at[chip], r.osem.at[N0], r.osem.at[N1], q)
-    loop(N64, send_back)
+        r.y_z[part, pl.ds(j4, N256, stride=N4), :] = r.xs_z[pl.ds(core * N2048 + j, N256, stride=N8), :] + y
+    for part in range(N2):
+        loop(N4, functools.partial(column, part))
+        r.send_o[part] = r.y_z[part].astype(BF16).reshape(N64, N16, N128)
+
+        def send_back(k0, part=part):
+            k = lax.rem(slot + N1 + k0, N64)
+            q = N64 * core + k
+
+            @pl.when(q != me)
+            def _():
+                send(r.send_o.at[part, k], r.recv_o.at[part, chip], r.osem.at[part], r.oarr.at[part], q)
+        loop(N64, send_back)
 
     @pl.when(mine)
     def _():
-        r.recv_o[chip] = r.send_o[slot]
+        for part in range(N2):
+            r.recv_o[part, chip] = r.send_o[part, slot]
     ga.sent()
     ready(mine, r.recv_m, N63, N64, r.am.at[N0])
     ready(mine, r.bias_s, N63, N64, r.ss)
@@ -609,28 +614,41 @@
     wait_bytes(r.zback.at[pl.ds(N0, N7)], r.bsem.at[N0])
     wait_bytes(r.mback.at[pl.ds(N0, N127)], r.msem.at[N0])
     wait_bytes(r.bias_e.at[pl.ds(N0, N63)], r.esem.at[N0])
-    ready(mine, r.recv_o, N63, N64, r.osem.at[N1])
-    got = r.recv_o[ALL].astype(F32).reshape(N64, N4, N8, N128)
+    wait_bytes(r.mback.at[pl.ds(N0, N127)], r.msem.at[N1])
+    put(r.yf_m, r.mback[ALL].astype(F32).reshape(N1024, N256))
+    for sl in range(N2):
+        for jl in range(N4):
+            spread(r.f_m, sl * N512 + jl, N128, N4, take(r.yf_m, sl * N4 + jl, N128, N8))
+    m_out[ALL] = join(r.f_m).astype(BF16).reshape(N2, N512, N256)
+
+    for part in range(N2):
+        ready(mine, r.recv_o.at[part], N63, N64, r.oarr.at[part])
+    for part in range(N2):
+        r.f_m[part] = r.recv_o[part].astype(F32).reshape(N1024, N128)
+        for il in range(N4):
+            for j4 in range(N4):
+                r.zf[il, pl.ds(N4 * part + j4, N64, stride=N8), :] = r.f_m[part, pl.ds(il * N4 + j4, N64, stride=N16), :]
     for il in range(N4):
-        z_out[il] = got[:, il].reshape(N512, N128).astype(BF16)
-    ready(mine, r.recv_o, N63, N64, r.osem.at[N0])
+        z_out[il] = r.zf[il].astype(BF16)
+    for part in range(N2):
+        ready(mine, r.recv_o.at[part], N63, N64, r.osem.at[part])
 
 
 BUFFERS = dict(
-    slab_a=(N32, N512), bias_a=(N64, N32, N512), xm=(N4, N512, N256), xn_m=(N512, N256), kv_m=(N4, N512, N512), q_m=(N4, N256, N256),
-    g_m=(N4, N256, N256), gt_m=(N4, N256, N256), rep8=(N512, N64), perm=(N256, N256), x_half=(N4, N256, N256), zsplit=(N8, N64, N512), zin=(N8, N64, N512), send_m=(N64, N16, N256),
-    recv_m=(N64, N16, N256), qkvg=(N256, N1024), left=(N4, N32, N256), right=(N4, N32, N256), lall=(N8, N4, N32, N256), rall=(N4, N16, N32, N256),
+    slab_a=(N32, N512), bias_a=(N64, N32, N512), xm=(N4, N512, N256), xn_m=(N512, N256), k_m=(N4, N512, N256), v_m=(N4, N256, N512), q_m=(N4, N256, N256),
+    g_m=(N2, N4, N256, N128), wrt=(N2, N256, N256), wct=(N2, N256, N256), perm=(N256, N256), x_half=(N4, N256, N256), zsplit=(N8, N64, N512), zin=(N8, N64, N512), send_m=(N64, N16, N256),
+    recv_m=(N64, N16, N256), left=(N4, N32, N256), right=(N4, N32, N256), lall=(N8, N4, N32, N256), rall=(N4, N16, N32, N256),
     mcols=(N128, N8, N256), o=(N4, N32, N64, N128), rc=(N32, N64, N256), mback=(N128, N8, N256), bd=(N16, N256, N512), zs=(N8, N64, N512), zback=(N8, N64, N512), zb=(N4, N512, N128),
     xz=(N8, N512, N128), slab_s=(N16, N512), bias_s=(N64, N16, N512), xn_z=(N512, N128), kv_z=(N8, N512, N256), q_z=(N8, N256, N128),
     g_z=(N8, N256, N128), gt_z=(N8, N256, N128), rep4=(N512, N128), wet=(N2, N128, N128), slab_e=(N32, N256),
     bias_e=(N64, N32, N256), send_zc=(N32, N64, N128), recv_zc=(N64, N64, N128), k_e=(N8, N512, N128), v_e=(N8, N128, N512), g_e=(N8, N128, N256),
-    send_o=(N64, N32, N128), recv_o=(N64, N32, N128))
+    send_o=(N2, N64, N16, N128), recv_o=(N2, N64, N16, N128))
 FLOATS = dict(
-    slab_f=(N32, N512), rmask=(N4, N512), cmask=(N4, N256), recip=(N8, N64, N4), hm8=(N512, N256), hm4=(N512, N128),
-    keepc=(N512, N128), keepr=(N1, N512), zf=(N4, N512, N128), pv=(N4, N2, N512, N128), y_m=(N2, N64, N128), f_b=(N2, N256, N128),
+    slab_f=(N32, N512), rmask=(N4, N512, N128), cmaskc=(N4, N256, N128), wide_a=(N4, N1024, N128), bias_t=(N8, N512, N128), cmask=(N4, N256), recip=(N8, N64, N4), hm4=(N512, N128),
+    keepc=(N512, N128), keepr=(N1, N512), zf=(N4, N512, N128), pv=(N4, N2, N512, N128), y_m=(N2, N128, N128), f_b=(N2, N512, N128),
     f_m=(N2, N1024, N128), xs_m=(N2, N1024, N128), yf_m=(N2, N1024, N128), wf=(N1024, N128), rf=(N2, N2048, N128), acc=(N256, N512),
-    e_f=(N32, N512), biasf=(N512, N512), f_z=(N32, N8, N8, N128), biasf_e=(N4, N512, N256), e_b=(N2, N32, N128), xs_z=(N4096, N128), y_z=(N2048, N128))
-SEMS = dict(a1=N2, a2=N2, az3=N2, ay3=N4, as1=None, as2=N2, as3=N2, gs=N2, ss=None, xsem=N2, ysem=N2, zsem=N2, am=N2, csem=N2, lsem=N2, bsem=N2, msem=N2, az=N2, fsem=N2, esem=N2, osem=N2)
+    e_f=(N32, N512), biasf=(N512, N512), f_z=(N32, N8, N8, N128), biasf_e=(N4, N512, N256), e_b=(N2, N32, N128), xs_z=(N4096, N128), y_z=(N2, N1024, N128))
+SEMS = dict(a1=N2, a2=N2, az3=N2, ay3=N4, as1=None, as2=N2, as3=N2, gs=N2, ss=None, xsem=N2, ysem=N2, zsem=N2, am=N2, csem=N2, lsem=N2, bsem=N2, msem=N2, az=N2, fsem=N2, esem=N2, osem=N2, oarr=N2)
 
 
 def solution(mesh):

time: 166 us -> 162 us (0.976)
  Pallas kernels: 162 us -> 159 us
    pallas_call x1, Pallas kernels: 162 us -> 159 us  [per_device(): pl.pallas_call(functools.partial(kernel, tuple(specs)), out_shape=(jax.Sh...]
where the time goes in v5:
time: 162 us
  Pallas kernels  159 us (98%)
  local copies, waits for them, and re-layouts  2.72 us (2%)
    pallas_call x1, Pallas kernels, per_device(): pl.pallas_call(functools.partial(kernel, tuple(specs)), out_shape=(jax.Sh...  159 us

profile of v5, /device:TPU:1, one launch (start us, length us, event | category | flops | bytes accessed | tf_op | source)
XLA Modules:
  0.0 162.2 jit_solution(820286878001060446)
XLA Ops:
  0.6 158.8 %shard_map.176 = (bf16[2,512,256]{2,1,0:T(8,128)(2,1)}, bf16[4,512,128]{2,1,0:T(8,128)(2,1)}) custom-call(bf16[2,512,256]{2,1,0:T(8,128)(2,1)} %m_ref.1, bf16[4,512,128]{2,1,0:T(8,128)(2,1)} %z_ref.1, s32[256,512]{1,0:T(8,128)} %mask_ref.1, s32[1,512]{1,0:T(1,128)} %bitcast.6, bf16[256,1024]{1,0:T(8,128)(2,1)} %w_row_in.1, bf16[8,128]{1,0:T(8,128)(2,1)} %bitcast.7, ...), custom_call_target="tpu_custom_call" | custom-call | tf_op jit(solution)/shard_map/pallas_call | solution.py:667
  159.5 0.0 copy-start
  159.5 1.9 %copy.21 = bf16[2,512,256]{2,1,0:T(8,128)(2,1)} copy(bf16[2,512,256]{2,1,0:T(8,128)(2,1)} %get-tuple-element.4) | data formatting | bytes 1048576
  161.4 0.0 copy-done
  161.4 0.8 copy.22
Async XLA Ops:
  159.5 1.9 %copy-start = (bf16[4,512,128]{2,1,0:T(8,128)(2,1)S(1)}, bf16[4,512,128]{2,1,0:T(8,128)(2,1)}, u32[]{:S(2)}) copy-start(bf16[4,512,128]{2,1,0:T(8,128)(2,1)} %get-tuple-element.5) | copy-start | bytes 1572868

commit v6 on v5

--- a/solution.py
+++ b/solution.py
@@ -336,7 +336,7 @@
             put(r.y_m, r.x_half[s, rows, :].astype(F32) + dot_c(gated, w_row_out[ALL], N0, N0))
             for jl in range(N4):
                 spread(r.f_b, s * N4 + jl, N32, N16, take(r.y_m, jl, N32, N4))
-        loop(N4, attend_m)
+        loop(N4, attend_m, N2)
         r.send_m[b * N32:(b + N1) * N32] = join(r.f_b).astype(BF16).reshape(N32, N16, N256)
 
         def send_cols_m(k0):
@@ -428,7 +428,7 @@
 
     def reorder(c):
         r.rc[c] = take(r.rf, c, N64, N32).astype(BF16)
-    loop(N32, reorder, N4)
+    loop(N32, reorder, N8)
 
     wait_bytes(r.zin.at[pl.ds(N0, N7)], r.zsem.at[N1])
 
@@ -436,7 +436,7 @@
         def outer(t):
             d = lax.rem(v + N1 + N4 * g + t, N8)
             r.o[t] = dot_t(r.rc[ALL].reshape(N2048, N256), r.lall[d].reshape(N128, N256)).astype(BF16).reshape(N32, N64, N128)
-        loop(N4, outer)
+        loop(N4, outer, N4)
 
         def mix(c4):
             total = None
@@ -445,7 +445,7 @@
                 part = dot(jnp.concatenate([r.o[:, c].reshape(N256, N128), r.o[:, c + N1].reshape(N256, N128)], axis=N1), r.bd[c4 * N4 + e])
                 total = part if total is None else total + part
             r.acc[ALL] = jnp.where(c4 == N0, 0.0, r.acc[ALL]) + total
-        loop(N4, mix)
+        loop(N4, mix, N2)
 
         def update(t):
             d = lax.rem(v + N1 + N4 * g + t, N8)
@@ -458,7 +458,7 @@
             @pl.when(d != v)
             def _():
                 send(r.zs.at[d], r.zback.at[v], r.bsem.at[N0], r.bsem.at[N1], u * N8 + d)
-        loop(N4, update)
+        loop(N4, update, N2)
     loop(N2, group)
     r.zback[v] = r.zs[v]
     wait_bytes(r.zback.at[pl.ds(N0, N7)], r.bsem.at[N1])
@@ -561,7 +561,7 @@
         xh = r.xn_z[hrows, :]
         r.q_z[j] = dot(xh, w_e_in[:, N0:N128]).astype(BF16)
         r.g_e[j] = dot_t(r.wet[N1], xh).astype(BF16)
-    loop(N8, project_e)
+    loop(N8, project_e, N2)
     wait_bytes(r.bias_e.at[pl.ds(N0, N63)], r.esem.at[N1])
 
     def widen(b):
@@ -585,7 +585,7 @@
         y = dot_c(gated, w_e_out[ALL], N0, N0)
         r.y_z[part, pl.ds(j4, N256, stride=N4), :] = r.xs_z[pl.ds(core * N2048 + j, N256, stride=N8), :] + y
     for part in range(N2):
-        loop(N4, functools.partial(column, part))
+        loop(N4, functools.partial(column, part), N4)
         r.send_o[part] = r.y_z[part].astype(BF16).reshape(N64, N16, N128)
 
         def send_back(k0, part=part):

time: 162 us -> 160 us (0.988)
  Pallas kernels: 159 us -> 156 us
    pallas_call x1, Pallas kernels: 159 us -> 156 us  [per_device(): pl.pallas_call(functools.partial(kernel, tuple(specs)), out_shape=(jax.Sh...]
where the time goes in v6:
time: 160 us
  Pallas kernels  156 us (98%)
  local copies, waits for them, and re-layouts  2.72 us (2%)
    pallas_call x1, Pallas kernels, per_device(): pl.pallas_call(functools.partial(kernel, tuple(specs)), out_shape=(jax.Sh...  156 us

profile of v6, /device:TPU:1, one launch (start us, length us, event | category | flops | bytes accessed | tf_op | source)
XLA Modules:
  0.0 159.6 jit_solution(16691240452831967836)
XLA Ops:
  0.6 156.2 %shard_map.176 = (bf16[2,512,256]{2,1,0:T(8,128)(2,1)}, bf16[4,512,128]{2,1,0:T(8,128)(2,1)}) custom-call(bf16[2,512,256]{2,1,0:T(8,128)(2,1)} %m_ref.1, bf16[4,512,128]{2,1,0:T(8,128)(2,1)} %z_ref.1, s32[256,512]{1,0:T(8,128)} %mask_ref.1, s32[1,512]{1,0:T(1,128)} %bitcast.6, bf16[256,1024]{1,0:T(8,128)(2,1)} %w_row_in.1, bf16[8,128]{1,0:T(8,128)(2,1)} %bitcast.7, ...), custom_call_target="tpu_custom_call" | custom-call | tf_op jit(solution)/shard_map/pallas_call | solution.py:667
  156.9 0.0 copy-start
  156.9 1.9 %copy.21 = bf16[2,512,256]{2,1,0:T(8,128)(2,1)} copy(bf16[2,512,256]{2,1,0:T(8,128)(2,1)} %get-tuple-element.4) | data formatting | bytes 1048576
  158.8 0.0 copy-done
  158.8 0.8 copy.22
Async XLA Ops:
  156.9 1.9 %copy-start = (bf16[4,512,128]{2,1,0:T(8,128)(2,1)S(1)}, bf16[4,512,128]{2,1,0:T(8,128)(2,1)}, u32[]{:S(2)}) copy-start(bf16[4,512,128]{2,1,0:T(8,128)(2,1)} %get-tuple-element.5) | copy-start | bytes 1572868
